TPU v7x, 128 devices: a whole 4x4x4 slice. The times are simulated.
128 devices in a mesh: gx: 8 (over z, core), gy: 4 (over y), gz: 4 (over x).
Axes of the slice: x: 4, y: 4, z: 4, core: 2. Of those that a mesh axis runs over, the one named last changes fastest.
Arguments:
- pressure_rhs: float32 [128, 128, 2048], P('gx', 'gy', 'gz'), may hold values from -6 to 6
- shift_diag: float32 [128, 128, 2048], P('gx', 'gy', 'gz'), may hold values from 0.02 to 0.3
- positions: float32 [3, 1048576], P(None, ('gx', 'gy', 'gz')), may hold values from -6 to 6
- normals: float32 [3, 1048576], P(None, ('gx', 'gy', 'gz')), may hold values from -6 to 6
- tension: float32 [1048576], P(('gx', 'gy', 'gz')), may hold values from 0.3 to 3
- edge_weight: float32 [6, 1048576], P(None, ('gx', 'gy', 'gz')), may hold values from 0.5 to 2
- owner_map: int32 [1048576, 1], P(('gx', 'gy', 'gz')), may hold values from 0 to 127; in each aligned block of 8192 rows (0 to 8191, 8192 to 16383, ...) at most 256 rows name the same one
- cell_map: int32 [1048576], P(('gx', 'gy', 'gz')), may hold values from 0 to 262143
- connectivity: int32 [6, 1048576], P(None, ('gx', 'gy', 'gz')), may hold values from 0 to 1048575, as said below
Outputs:
- pressure: float32 [128, 128, 2048], P('gx', 'gy', 'gz')
- surface_force: float32 [3, 1048576], P(None, ('gx', 'gy', 'gz'))
Inputs may be any that keep to these rules, and one draw needn't show every extreme that they name: `connectivity`: each neighbour index differs from the point's own index by 1 to 64, counted cyclically over 1048576; the distance 64 occurs. `owner_map`: among the points of one device no owner is named more than 256 times, a bound that some block reaches.
All inputs are finite; a program needn't handle non-finite values.
Results may differ from a plain program's by a relative error of at most 0.0003.
Values sent between devices are 32-bit elements; how exact they have to be, the bound alone decides.
A program may use at most 192 MiB of HBM per device.

v0:
```python
import jax
import jax.numpy as jnp
from jax import lax
from jax.sharding import PartitionSpec as P

HALO = 64
SMOOTH = 3
COARSE_SMOOTH = 4


centre = 1.125
spread = 0.875


def extended(value, sides, width):
    edges = {}
    for axis, dim in sides:
        devices, length = (lax.axis_size(axis), value.shape[dim])
        up = [(i, (i + 1) % devices) for i in range(devices - 1)]
        last = lax.slice_in_dim(value, length - width, length, axis=dim)
        initial = lax.slice_in_dim(value, 0, width, axis=dim)
        edges[dim] = (
            lax.ppermute(last, axis, up),
            lax.ppermute(initial, axis, [(b, a) for a, b in up]),
        )
    done = []
    for _, dim in sides:
        low, high = edges[dim]
        around = [(width, width) if d in done else (0, 0) for d in range(value.ndim)]
        value = jnp.concatenate([jnp.pad(low, around), value, jnp.pad(high, around)], axis=dim)
        done.append(dim)
    return value


def padded_2(cells, sides, width, closed):
    for axis, dim in sides:
        count = lax.axis_size(axis)
        ends = count if closed else count - 1
        head = lax.slice_in_dim(cells, 0, width, axis=dim)
        tail = lax.slice_in_dim(cells, cells.shape[dim] - width, cells.shape[dim], axis=dim)
        cells = jnp.concatenate(
            [
                lax.ppermute(tail, axis, [(i, (i + 1) % count) for i in range(ends)]),
                cells,
                lax.ppermute(head, axis, [((i + 1) % count, i) for i in range(ends)]),
            ],
            axis=dim,
        )
    return cells


def side_by_side(arrays, axis, split_dim, concat_dim, along):
    both = jnp.concatenate(arrays, axis=along)
    filled, at, outs = (
        lax.all_to_all(both, axis, split_axis=split_dim, concat_axis=concat_dim, tiled=True),
        0,
        [],
    )
    for a in arrays:
        outs.append(lax.slice_in_dim(filled, at, at + a.shape[along], axis=along))
        at += a.shape[along]
    return tuple(outs)


def stencil(padded, field, shift):
    beside = padded[2:, 1:-1, 1:-1] + padded[:-2, 1:-1, 1:-1]
    beside = beside + padded[1:-1, 2:, 1:-1] + padded[1:-1, :-2, 1:-1]
    beside = beside + padded[1:-1, 1:-1, 2:] + padded[1:-1, 1:-1, :-2]
    return (6.0 + shift) * field - beside


def coarse_apply(field, shift):
    padded = extended(field, (("gx", 0), ("gy", 1), ("gz", 2)), 1)
    return stencil(padded, field, shift)


def local_apply(field, shift):
    return stencil(jnp.pad(field, 1), field, shift)


def chebyshev(target, shift, start, sweeps, apply_fn, inside):
    inverse = 1.0 / (6.0 + shift)
    ratio = centre / spread
    factor = 1.0 / ratio
    if start is None:
        update = inverse * target / centre
        answer = update
    else:
        update = inverse * (target - apply_fn(start, shift)) / centre
        update = update * inside
        answer = start + update
    for sweep in range(1, sweeps):
        remain = inverse * (target - apply_fn(answer, shift))
        if inside is not None:
            remain = remain * inside
        factor_new = 1.0 / (2.0 * ratio - factor)
        update = factor_new * factor * update + 2.0 * factor_new / spread * remain
        answer = answer + update
        factor = factor_new
    return answer


def domain_mask(shape, width):
    places = (lax.axis_index("gx"), lax.axis_index("gy"), lax.axis_index("gz"))
    counts = (lax.axis_size("gx"), lax.axis_size("gy"), lax.axis_size("gz"))
    factors = []
    for which in range(3):
        length = shape[which]
        where = places[which] * length - width + jnp.arange(length + 2 * width, dtype=jnp.int32)
        factors.append(((where >= 0) & (where < length * counts[which])).astype(jnp.float32))
    return factors[0][:, None, None] * factors[1][None, :, None] * factors[2][None, None, :]


def interior(field, width):
    return field[width:-width, width:-width, width:-width]


def blocks(field):
    return field.reshape(field.shape[0] // 2, 2, field.shape[1] // 2, 2, field.shape[2] // 2, 2)


def gather_neighbours(padded, relative, npoint):
    block_len = 2 * HALO
    nblock = npoint // block_len
    lower = padded[:, :npoint].reshape(3, nblock, block_len)
    upper = padded[:, block_len:].reshape(3, nblock, block_len)
    window = jnp.concatenate([lower, upper], axis=2)
    starts = (jnp.arange(nblock, dtype=jnp.int32) * block_len)[None, :, None]
    local_idx = relative.reshape(relative.shape[0], nblock, block_len) - starts
    columns = jnp.arange(2 * block_len, dtype=jnp.int32)
    picked = []
    for which in range(relative.shape[0]):
        select = (local_idx[which][:, :, None] == columns[None, None, :]).astype(jnp.float32)
        taken = jnp.einsum("bpw,cbw->cbp", select, window, precision=lax.Precision.HIGHEST)
        picked.append(taken.reshape(3, npoint))
    return jnp.stack(picked, axis=1)


def slot_ranks(owner_ids, ndevice, npoint):
    block_len = 2 * HALO
    nblock = npoint // block_len
    owner_hot = (owner_ids[:, None] == jnp.arange(ndevice, dtype=jnp.int32)[None, :]).astype(
        jnp.bfloat16
    )
    owner_blocks = owner_hot.reshape(nblock, block_len, ndevice)
    lower_tri = (jnp.arange(block_len)[:, None] > jnp.arange(block_len)[None, :]).astype(
        jnp.bfloat16
    )
    within = jnp.einsum("pq,bqo->bpo", lower_tri, owner_blocks, preferred_element_type=jnp.float32)
    counts = jnp.sum(owner_blocks.astype(jnp.float32), axis=1)
    before = jnp.cumsum(counts, axis=0) - counts
    ranks = jnp.sum((within + before[:, None, :]) * owner_blocks.astype(jnp.float32), axis=2)
    return (ranks.reshape(npoint).astype(jnp.int32), owner_hot)


def body(
    pressure_rhs,
    shift_diag,
    positions,
    normals,
    tension,
    edge_weight,
    owner_map,
    cell_map,
    connectivity,
):
    npoint = positions.shape[1]
    ndevice = lax.axis_size(("gx", "gy", "gz"))
    total = npoint * ndevice
    begin = lax.axis_index(("gx", "gy", "gz")) * npoint
    padded = padded_2(positions, ((("gx", "gy", "gz"), 1),), HALO, True)
    relative = (connectivity - begin + HALO + total) % total
    neighbours = gather_neighbours(padded, relative, npoint)
    surface_force = tension[None, :] * jnp.sum(
        edge_weight[None, :, :] * (neighbours - positions[:, None, :]), axis=1
    )
    jump = jnp.sum(surface_force * normals, axis=0)
    owner_ids = owner_map[:, 0]
    capacity = 4 * npoint // ndevice
    ranks, owner_hot = slot_ranks(owner_ids, ndevice, npoint)
    rank_hot = (ranks[:, None] == jnp.arange(capacity, dtype=jnp.int32)[None, :]).astype(
        jnp.float32
    )
    carried = jnp.stack([jump, cell_map.astype(jnp.float32)], axis=0)
    weighted = carried[:, :, None] * rank_hot[None, :, :]
    packed = jnp.einsum(
        "po,kpr->kor", owner_hot.astype(jnp.float32), weighted, precision=lax.Precision.HIGHEST
    )
    values = packed[0]
    cell_ids = packed[1]
    got_values, got_cells = side_by_side((values, cell_ids), ("gx", "gy", "gz"), 0, 0, 1)
    shape = pressure_rhs.shape
    source = jnp.zeros((shape[0] * shape[1] * shape[2],), jnp.float32)
    source = source.at[got_cells.reshape(-1).astype(jnp.int32)].add(got_values.reshape(-1))
    forcing = pressure_rhs + source.reshape(shape)
    coarse_shift = 4.0 * jnp.mean(blocks(shift_diag), axis=(1, 3, 5))
    width = SMOOTH
    inside = domain_mask(shape, width)
    forcing_wide, shift_wide = (
        padded_2(forcing, (("gx", 0), ("gy", 1), ("gz", 2)), width, False),
        padded_2(shift_diag, (("gx", 0), ("gy", 1), ("gz", 2)), width, False),
    )
    smooth_wide = chebyshev(forcing_wide, shift_wide, None, SMOOTH, local_apply, inside)
    remain = interior(forcing_wide - local_apply(smooth_wide, shift_wide), width)
    smooth = interior(smooth_wide, width)
    coarse_rhs = 0.5 * jnp.sum(blocks(remain), axis=(1, 3, 5))
    coarse_fix = chebyshev(coarse_rhs, coarse_shift, None, COARSE_SMOOTH, coarse_apply, None)
    spreadout = jnp.broadcast_to(
        coarse_fix[:, None, :, None, :, None], blocks(shift_diag).shape
    ).reshape(shape)
    start_wide = padded_2(smooth + spreadout, (("gx", 0), ("gy", 1), ("gz", 2)), width, False)
    pressure = interior(
        chebyshev(forcing_wide, shift_wide, start_wide, SMOOTH, local_apply, inside), width
    )
    return (pressure, surface_force)


def solution(mesh):
    return jax.shard_map(
        body,
        mesh=mesh,
        in_specs=(
            P("gx", "gy", "gz"),
            P("gx", "gy", "gz"),
            P(None, ("gx", "gy", "gz")),
            P(None, ("gx", "gy", "gz")),
            P(("gx", "gy", "gz")),
            P(None, ("gx", "gy", "gz")),
            P(("gx", "gy", "gz"), None),
            P(("gx", "gy", "gz")),
            P(None, ("gx", "gy", "gz")),
        ),
        out_specs=(P("gx", "gy", "gz"), P(None, ("gx", "gy", "gz"))),
        check_vma=False,
    )
```

profile of v0, /device:TPU:1, one launch (start us, length us, event | category | flops | bytes accessed | tf_op | source)
XLA Modules:
  0.0 726.9 jit_solution(6783575048737289273)
XLA Ops:
  3.4 4.3 collective-permute-start.7
  8.8 5.2 collective-permute-start.1
  20.3 4.3 fusion.10
  24.9 4.3 fusion.7
  29.3 4.4 fusion.6
  33.6 4.4 fusion.5
  38.0 4.4 fusion.4
  42.4 4.4 fusion.3
  46.8 4.8 fusion.2
  52.7 8.6 %fusion.46 = f32[2,128,256]{1,2,0:T(8,128)S(1)} fusion(s32[8192]{0:T(1024)S(1)} %bitcast.104, f32[8192,256]{0,1:T(8,128)S(1)} %bitcast.95, f32[2,8192]{1,0:T(2,128)S(1)} %pad_maximum_fusion.72), kind=kOutput, calls=%fused_computation.98 | convolution fusion | flops 6447693824 | bytes 8749056 | tf_op jit(solution)/shard_map/po,kpr->kor/dot_general | solution.py:186
  62.2 5.1 all-to-all-start
  67.5 11.1 %all-to-all-done = f32[128,1,512]{2,1,0:T(1,128)S(1)} async-done(((f32[128,1,512]{2,1,0:T(1,128)}), f32[128,1,512]{2,1,0:T(1,128)S(1)}, u32[]{:S(2)}, u32[]{:S(2)}) %all-to-all-start) | async-done | bytes 262176 | tf_op jit(solution)/shard_map/all_to_all | solution.py:55
  78.9 202.6 %scatter_custom_fusion = f32[262144]{0:T(1024)S(1)} fusion(s32[32768]{0:T(1024)S(1)} %bitcast.100, f32[32768]{0:T(1024)S(1)} %bitcast.99, f32[]{:T(128)} %constant.31.clone.1), kind=kCustom, calls=%fused_computation.118 | custom fusion | flops 32768 | bytes 1048580 | tf_op jit(solution)/shard_map/scatter-add | solution.py:194
  285.2 20.0 %collective-permute-start.8 = (f32[3,32,512]{2,1,0:T(8,128)}, f32[3,32,512]{2,1,0:T(8,128)S(1)}, u32[]{:S(2)}, u32[]{:S(2)}) collective-permute-start(f32[3,32,512]{2,1,0:T(8,128)} %get-tuple-element.37), channel_id=1, source_target_pairs={{0,16},{16,32},{32,48},{48,64},{64,80},{80,96},{96,112},{1,17},{17... | collective-permute-start | bytes 589832 | tf_op jit(solution)/shard_map/ppermute | solution.py:43
  311.7 69.1 %reshape.180 = f32[8,2,16,2,256,2]{5,4,3,2,1,0:T(8,128)} reshape(f32[16,32,512]{2,1,0:T(8,128)} %param.10) | data formatting | bytes 2097152 | tf_op jit(solution)/shard_map/reshape | solution.py:119
  380.9 20.8 %reduce_sum.58 = f32[8,16,256]{2,1,0:T(8,128)S(1)} reduce(f32[8,2,16,2,256,2]{5,4,3,2,1,0:T(8,128)} %reshape.180, f32[]{:T(128)} %constant.31.clone.1), dimensions={1,3,5}, to_apply=%region_6.7 | reduce | flops 229376 | bytes 1179652 | tf_op jit(solution)/shard_map/reduce_sum | solution.py:196
  413.8 4.5 collective-permute-start.12
  446.6 68.4 %reshape.181 = f32[8,2,16,2,256,2]{5,4,3,2,1,0:T(8,128)} reshape(f32[16,32,512]{2,1,0:T(8,128)S(1)} %fusion.54) | data formatting | bytes 2097152 | tf_op jit(solution)/shard_map/reshape | solution.py:119
  515.0 20.8 %reduce_sum.59 = f32[8,16,256]{2,1,0:T(8,128)S(1)} reduce(f32[8,2,16,2,256,2]{5,4,3,2,1,0:T(8,128)} %reshape.181, f32[]{:T(128)} %constant.31.clone.1), dimensions={1,3,5}, to_apply=%region_7.8 | reduce | flops 229376 | bytes 1179652 | tf_op jit(solution)/shard_map/reduce_sum | solution.py:206
  558.6 5.0 collective-permute-start.21
  566.9 4.6 collective-permute-start.25
  578.6 4.8 collective-permute-start.27
  586.7 4.8 collective-permute-start.31
  592.9 21.4 %broadcast_in_dim.5 = f32[8,2,16,2,256,2]{5,4,3,2,1,0:T(8,128)} broadcast(f32[8,16,256]{2,1,0:T(8,128)S(1)} %fusion.66), dimensions={0,2,4} | broadcast | bytes 1179648 | tf_op jit(solution)/shard_map/broadcast_in_dim | solution.py:208
  614.3 47.0 %reshape.182 = f32[16,32,512]{2,1,0:T(8,128)S(1)} reshape(f32[8,2,16,2,256,2]{5,4,3,2,1,0:T(8,128)} %broadcast_in_dim.5) | data formatting | bytes 2097152 | tf_op jit(solution)/shard_map/reshape | solution.py:210
  663.2 4.5 collective-permute-start.32
  670.3 4.4 collective-permute-done.33
  674.8 4.3 collective-permute-start.34
  691.0 6.9 collective-permute-done.36
  705.9 4.4 fusion.106
  710.3 9.2 %add_subtract_fusion = f32[22,38,518]{2,1,0:T(8,128)} fusion(f32[22,38,518]{2,1,0:T(8,128)} %get-tuple-element.4, f32[22,38,518]{2,1,0:T(8,128)S(1)} %get-tuple-element.3), kind=kLoop, calls=%fused_computation.53 | loop fusion | flops 3031336 | bytes 5196576 | tf_op jit(solution)/shard_map/sub | solution.py:69
  719.6 7.1 slice_add_fusion.1
  (176 shorter events, 125.0 us)
Async XLA Ops:
  1.4 23.3 %collective-permute-start.6 = (f32[3,64]{1,0:T(4,128)S(1)}, f32[3,64]{1,0:T(4,128)S(1)}, u32[]{:S(2)}, u32[]{:S(2)}) collective-permute-start(f32[3,64]{1,0:T(4,128)S(1)} %get-tuple-element.71), channel_id=1, source_target_pairs={{0,1},{1,2},{2,3},{3,4},{4,5},{5,6},{6,7},{7,8},{8,9},{9,10},{10,1... | collective-permute-start | bytes 2312 | tf_op jit(solution)/shard_map/ppermute | solution.py:43
  3.4 21.3 %collective-permute-start.7 = (f32[3,64]{1,0:T(4,128)S(1)}, f32[3,64]{1,0:T(4,128)S(1)}, u32[]{:S(2)}, u32[]{:S(2)}) collective-permute-start(f32[3,64]{1,0:T(4,128)S(1)} %get-tuple-element.72), channel_id=1, source_target_pairs={{1,0},{2,1},{3,2},{4,3},{5,4},{6,5},{7,6},{8,7},{9,8},{10,9},{11,1... | collective-permute-start | bytes 2312 | tf_op jit(solution)/shard_map/ppermute | solution.py:45
  8.8 58.7 %collective-permute-start.1 = (f32[3,32,512]{2,1,0:T(8,128)S(1)}, f32[3,32,512]{2,1,0:T(8,128)S(1)}, u32[]{:S(2)}, u32[]{:S(2)}) collective-permute-start(f32[3,32,512]{2,1,0:T(8,128)S(1)} %get-tuple-element.39), channel_id=1, source_target_pairs={{16,0},{32,16},{48,32},{64,48},{80,64},{96,80},{112,96},{17,1},{33... | collective-permute-start | bytes 589832 | tf_op jit(solution)/shard_map/ppermute | solution.py:45
  14.0 53.3 %collective-permute-start = (f32[3,32,512]{2,1,0:T(8,128)S(1)}, f32[3,32,512]{2,1,0:T(8,128)S(1)}, u32[]{:S(2)}, u32[]{:S(2)}) collective-permute-start(f32[3,32,512]{2,1,0:T(8,128)S(1)} %get-tuple-element.40), channel_id=1, source_target_pairs={{0,16},{16,32},{32,48},{48,64},{64,80},{80,96},{96,112},{1,17},{17... | collective-permute-start | bytes 589832 | tf_op jit(solution)/shard_map/ppermute | solution.py:43
  62.2 16.3 %all-to-all-start = ((f32[128,1,512]{2,1,0:T(1,128)}), f32[128,1,512]{2,1,0:T(1,128)S(1)}, u32[]{:S(2)}, u32[]{:S(2)}) async-start(f32[128,1,512]{2,1,0:T(1,128)} %copy.13), calls=%async_computation | async-start | bytes 524288 | tf_op jit(solution)/shard_map/all_to_all | solution.py:55
  285.2 116.5 %collective-permute-start.8 = (f32[3,32,512]{2,1,0:T(8,128)}, f32[3,32,512]{2,1,0:T(8,128)S(1)}, u32[]{:S(2)}, u32[]{:S(2)}) collective-permute-start(f32[3,32,512]{2,1,0:T(8,128)} %get-tuple-element.37), channel_id=1, source_target_pairs={{0,16},{16,32},{32,48},{48,64},{64,80},{80,96},{96,112},{1,17},{17... | collective-permute-start | bytes 589832 | tf_op jit(solution)/shard_map/ppermute | solution.py:43
  305.2 96.5 %collective-permute-start.9 = (f32[3,32,512]{2,1,0:T(8,128)}, f32[3,32,512]{2,1,0:T(8,128)S(1)}, u32[]{:S(2)}, u32[]{:S(2)}) collective-permute-start(f32[3,32,512]{2,1,0:T(8,128)} %get-tuple-element.38), channel_id=1, source_target_pairs={{16,0},{32,16},{48,32},{64,48},{80,64},{96,80},{112,96},{17,1},{33... | collective-permute-start | bytes 589832 | tf_op jit(solution)/shard_map/ppermute | solution.py:45
  308.9 98.2 %collective-permute-start.2 = (f32[22,3,512]{2,1,0:T(4,128)}, f32[22,3,512]{2,1,0:T(4,128)S(1)}, u32[]{:S(2)}, u32[]{:S(2)}) collective-permute-start(f32[22,3,512]{2,1,0:T(4,128)} %get-tuple-element.33), channel_id=1, source_target_pairs={{0,4},{4,8},{8,12},{1,5},{5,9},{9,13},{2,6},{6,10},{10,14},{3,7},{... | collective-permute-start | bytes 405512 | tf_op jit(solution)/shard_map/ppermute | solution.py:43
  310.4 96.7 %collective-permute-start.3 = (f32[22,3,512]{2,1,0:T(4,128)}, f32[22,3,512]{2,1,0:T(4,128)S(1)}, u32[]{:S(2)}, u32[]{:S(2)}) collective-permute-start(f32[22,3,512]{2,1,0:T(4,128)} %get-tuple-element.34), channel_id=1, source_target_pairs={{4,0},{8,4},{12,8},{5,1},{9,5},{13,9},{6,2},{10,6},{14,10},{7,3},{... | collective-permute-start | bytes 405512 | tf_op jit(solution)/shard_map/ppermute | solution.py:45
  401.8 10.9 %collective-permute-start.10 = (f32[22,3,512]{2,1,0:T(4,128)S(1)}, f32[22,3,512]{2,1,0:T(4,128)S(1)}, u32[]{:S(2)}, u32[]{:S(2)}) collective-permute-start(f32[22,3,512]{2,1,0:T(4,128)S(1)} %get-tuple-element.31), channel_id=1, source_target_pairs={{0,4},{4,8},{8,12},{1,5},{5,9},{9,13},{2,6},{6,10},{10,14},{3,7},{... | collective-permute-start | bytes 405512 | tf_op jit(solution)/shard_map/ppermute | solution.py:43
  405.8 7.8 %collective-permute-start.11 = (f32[22,3,512]{2,1,0:T(4,128)S(1)}, f32[22,3,512]{2,1,0:T(4,128)S(1)}, u32[]{:S(2)}, u32[]{:S(2)}) collective-permute-start(f32[22,3,512]{2,1,0:T(4,128)S(1)} %get-tuple-element.32), channel_id=1, source_target_pairs={{4,0},{8,4},{12,8},{5,1},{9,5},{13,9},{6,2},{10,6},{14,10},{7,3},{... | collective-permute-start | bytes 405512 | tf_op jit(solution)/shard_map/ppermute | solution.py:45
  407.4 14.1 %collective-permute-start.4 = (f32[22,38,3]{2,1,0:T(8,128)S(1)}, f32[22,38,3]{2,1,0:T(8,128)S(1)}, u32[]{:S(2)}, u32[]{:S(2)}) collective-permute-start(f32[22,38,3]{2,1,0:T(8,128)S(1)} %get-tuple-element.27), channel_id=1, source_target_pairs={{0,1},{1,2},{2,3},{4,5},{5,6},{6,7},{8,9},{9,10},{10,11},{12,13},{... | collective-permute-start | bytes 30104 | tf_op jit(solution)/shard_map/ppermute | solution.py:43
  411.3 14.0 %collective-permute-start.5 = (f32[22,38,3]{2,1,0:T(8,128)S(1)}, f32[22,38,3]{2,1,0:T(8,128)S(1)}, u32[]{:S(2)}, u32[]{:S(2)}) collective-permute-start(f32[22,38,3]{2,1,0:T(8,128)S(1)} %get-tuple-element.28), channel_id=1, source_target_pairs={{1,0},{2,1},{3,2},{5,4},{6,5},{7,6},{9,8},{10,9},{11,10},{13,12},{... | collective-permute-start | bytes 30104 | tf_op jit(solution)/shard_map/ppermute | solution.py:45
  413.8 17.3 %collective-permute-start.12 = (f32[22,38,3]{2,1,0:T(8,128)S(1)}, f32[22,38,3]{2,1,0:T(8,128)S(1)}, u32[]{:S(2)}, u32[]{:S(2)}) collective-permute-start(f32[22,38,3]{2,1,0:T(8,128)S(1)} %get-tuple-element.25), channel_id=1, source_target_pairs={{0,1},{1,2},{2,3},{4,5},{5,6},{6,7},{8,9},{9,10},{10,11},{12,13},{... | collective-permute-start | bytes 30104 | tf_op jit(solution)/shard_map/ppermute | solution.py:43
  418.4 16.6 %collective-permute-start.13 = (f32[22,38,3]{2,1,0:T(8,128)S(1)}, f32[22,38,3]{2,1,0:T(8,128)S(1)}, u32[]{:S(2)}, u32[]{:S(2)}) collective-permute-start(f32[22,38,3]{2,1,0:T(8,128)S(1)} %get-tuple-element.26), channel_id=1, source_target_pairs={{1,0},{2,1},{3,2},{5,4},{6,5},{7,6},{9,8},{10,9},{11,10},{13,12},{... | collective-permute-start | bytes 30104 | tf_op jit(solution)/shard_map/ppermute | solution.py:45
  535.8 11.5 %collective-permute-start.17 = (f32[8,1,256]{2,1,0:T(1,128)S(1)}, f32[8,1,256]{2,1,0:T(1,128)S(1)}, u32[]{:S(2)}, u32[]{:S(2)}) collective-permute-start(f32[8,1,256]{2,1,0:T(1,128)S(1)} %get-tuple-element.65), channel_id=1, source_target_pairs={{0,4},{4,8},{8,12},{1,5},{5,9},{9,13},{2,6},{6,10},{10,14},{3,7},{... | collective-permute-start | bytes 24584 | tf_op jit(solution)/shard_map/ppermute | solution.py:23
  539.6 11.8 %collective-permute-start.16 = (f32[8,1,256]{2,1,0:T(1,128)S(1)}, f32[8,1,256]{2,1,0:T(1,128)S(1)}, u32[]{:S(2)}, u32[]{:S(2)}) collective-permute-start(f32[8,1,256]{2,1,0:T(1,128)S(1)} %get-tuple-element.66), channel_id=1, source_target_pairs={{4,0},{8,4},{12,8},{5,1},{9,5},{13,9},{6,2},{10,6},{14,10},{7,3},{... | collective-permute-start | bytes 24584 | tf_op jit(solution)/shard_map/ppermute | solution.py:24
  540.9 11.9 %collective-permute-start.15 = (f32[1,16,256]{2,1,0:T(8,128)S(1)}, f32[1,16,256]{2,1,0:T(8,128)S(1)}, u32[]{:S(2)}, u32[]{:S(2)}) collective-permute-start(f32[1,16,256]{2,1,0:T(8,128)S(1)} %get-tuple-element.67), channel_id=1, source_target_pairs={{0,16},{16,32},{32,48},{48,64},{64,80},{80,96},{96,112},{1,17},{17... | collective-permute-start | bytes 49160 | tf_op jit(solution)/shard_map/ppermute | solution.py:23
  544.0 8.7 %collective-permute-start.14 = (f32[1,16,256]{2,1,0:T(8,128)S(1)}, f32[1,16,256]{2,1,0:T(8,128)S(1)}, u32[]{:S(2)}, u32[]{:S(2)}) collective-permute-start(f32[1,16,256]{2,1,0:T(8,128)S(1)} %get-tuple-element.68), channel_id=1, source_target_pairs={{16,0},{32,16},{48,32},{64,48},{80,64},{96,80},{112,96},{17,1},{33... | collective-permute-start | bytes 49160 | tf_op jit(solution)/shard_map/ppermute | solution.py:24
  553.0 13.9 %collective-permute-start.23 = (f32[8,1,256]{2,1,0:T(1,128)S(1)}, f32[8,1,256]{2,1,0:T(1,128)S(1)}, u32[]{:S(2)}, u32[]{:S(2)}) collective-permute-start(f32[8,1,256]{2,1,0:T(1,128)S(1)} %get-tuple-element.59), channel_id=1, source_target_pairs={{0,4},{4,8},{8,12},{1,5},{5,9},{9,13},{2,6},{6,10},{10,14},{3,7},{... | collective-permute-start | bytes 24584 | tf_op jit(solution)/shard_map/ppermute | solution.py:23
  557.3 14.2 %collective-permute-start.22 = (f32[8,1,256]{2,1,0:T(1,128)S(1)}, f32[8,1,256]{2,1,0:T(1,128)S(1)}, u32[]{:S(2)}, u32[]{:S(2)}) collective-permute-start(f32[8,1,256]{2,1,0:T(1,128)S(1)} %get-tuple-element.60), channel_id=1, source_target_pairs={{4,0},{8,4},{12,8},{5,1},{9,5},{13,9},{6,2},{10,6},{14,10},{7,3},{... | collective-permute-start | bytes 24584 | tf_op jit(solution)/shard_map/ppermute | solution.py:24
  558.6 14.2 %collective-permute-start.21 = (f32[1,16,256]{2,1,0:T(8,128)S(1)}, f32[1,16,256]{2,1,0:T(8,128)S(1)}, u32[]{:S(2)}, u32[]{:S(2)}) collective-permute-start(f32[1,16,256]{2,1,0:T(8,128)S(1)} %get-tuple-element.61), channel_id=1, source_target_pairs={{0,16},{16,32},{32,48},{48,64},{64,80},{80,96},{96,112},{1,17},{17... | collective-permute-start | bytes 49160 | tf_op jit(solution)/shard_map/ppermute | solution.py:23
  563.5 9.3 %collective-permute-start.20 = (f32[1,16,256]{2,1,0:T(8,128)S(1)}, f32[1,16,256]{2,1,0:T(8,128)S(1)}, u32[]{:S(2)}, u32[]{:S(2)}) collective-permute-start(f32[1,16,256]{2,1,0:T(8,128)S(1)} %get-tuple-element.62), channel_id=1, source_target_pairs={{16,0},{32,16},{48,32},{64,48},{80,64},{96,80},{112,96},{17,1},{33... | collective-permute-start | bytes 49160 | tf_op jit(solution)/shard_map/ppermute | solution.py:24
  573.1 13.7 %collective-permute-start.29 = (f32[8,1,256]{2,1,0:T(1,128)S(1)}, f32[8,1,256]{2,1,0:T(1,128)S(1)}, u32[]{:S(2)}, u32[]{:S(2)}) collective-permute-start(f32[8,1,256]{2,1,0:T(1,128)S(1)} %get-tuple-element.55), channel_id=1, source_target_pairs={{0,4},{4,8},{8,12},{1,5},{5,9},{9,13},{2,6},{6,10},{10,14},{3,7},{... | collective-permute-start | bytes 24584 | tf_op jit(solution)/shard_map/ppermute | solution.py:23
  577.3 14.3 %collective-permute-start.28 = (f32[8,1,256]{2,1,0:T(1,128)S(1)}, f32[8,1,256]{2,1,0:T(1,128)S(1)}, u32[]{:S(2)}, u32[]{:S(2)}) collective-permute-start(f32[8,1,256]{2,1,0:T(1,128)S(1)} %get-tuple-element.56), channel_id=1, source_target_pairs={{4,0},{8,4},{12,8},{5,1},{9,5},{13,9},{6,2},{10,6},{14,10},{7,3},{... | collective-permute-start | bytes 24584 | tf_op jit(solution)/shard_map/ppermute | solution.py:24
  578.6 14.0 %collective-permute-start.27 = (f32[1,16,256]{2,1,0:T(8,128)S(1)}, f32[1,16,256]{2,1,0:T(8,128)S(1)}, u32[]{:S(2)}, u32[]{:S(2)}) collective-permute-start(f32[1,16,256]{2,1,0:T(8,128)S(1)} %get-tuple-element.53), channel_id=1, source_target_pairs={{0,16},{16,32},{32,48},{48,64},{64,80},{80,96},{96,112},{1,17},{17... | collective-permute-start | bytes 49160 | tf_op jit(solution)/shard_map/ppermute | solution.py:23
  583.4 9.3 %collective-permute-start.26 = (f32[1,16,256]{2,1,0:T(8,128)S(1)}, f32[1,16,256]{2,1,0:T(8,128)S(1)}, u32[]{:S(2)}, u32[]{:S(2)}) collective-permute-start(f32[1,16,256]{2,1,0:T(8,128)S(1)} %get-tuple-element.54), channel_id=1, source_target_pairs={{16,0},{32,16},{48,32},{64,48},{80,64},{96,80},{112,96},{17,1},{33... | collective-permute-start | bytes 49160 | tf_op jit(solution)/shard_map/ppermute | solution.py:24
  663.2 7.1 collective-permute-start.32
  667.7 7.0 collective-permute-start.33
  674.8 6.7 collective-permute-start.34
  685.6 12.4 %collective-permute-start.36 = (f32[22,38,3]{2,1,0:T(8,128)S(1)}, f32[22,38,3]{2,1,0:T(8,128)S(1)}, u32[]{:S(2)}, u32[]{:S(2)}) collective-permute-start(f32[22,38,3]{2,1,0:T(8,128)S(1)} %get-tuple-element.23), channel_id=1, source_target_pairs={{0,1},{1,2},{2,3},{4,5},{5,6},{6,7},{8,9},{9,10},{10,11},{12,13},{... | collective-permute-start | bytes 30104 | tf_op jit(solution)/shard_map/ppermute | solution.py:43
  689.6 12.6 %collective-permute-start.37 = (f32[22,38,3]{2,1,0:T(8,128)S(1)}, f32[22,38,3]{2,1,0:T(8,128)S(1)}, u32[]{:S(2)}, u32[]{:S(2)}) collective-permute-start(f32[22,38,3]{2,1,0:T(8,128)S(1)} %get-tuple-element.24), channel_id=1, source_target_pairs={{1,0},{2,1},{3,2},{5,4},{6,5},{7,6},{9,8},{10,9},{11,10},{13,12},{... | collective-permute-start | bytes 30104 | tf_op jit(solution)/shard_map/ppermute | solution.py:45
  (28 other events, 573.0 us)
where the time goes:
time: 737 us; the launch traced here: 727 us
  other arithmetic  296 us (40%)
  local copies, waits for them, and re-layouts  212 us (29%)
  starting transfers between devices  130 us (18%)
  waiting for transfers between devices  48.5 us (7%)
  matrix products  37.7 us (5%)
    scatter-add x1, other arithmetic, body(): source.at[got_cells.reshape(-1).astype(jnp.int32)]  203 us
    reshape x2, local copies, waits for them, and re-layouts, blocks(): field.reshape(field.shape[0] // 2, 2, field.shape[1] // 2, 2, field.shape...  138 us
    ppermute x10, starting transfers between devices, padded_2(): lax.ppermute(tail, axis, [(i, (i + 1) % count) for i in range(ends)])  50.7 us
    reshape x1, local copies, waits for them, and re-layouts, body(): spreadout = jnp.broadcast_to(coarse_fix[:, None, :, None, :, None], block...  47 us
    ppermute x9, starting transfers between devices, extended(): lax.ppermute(last, axis, up)  38.6 us
    dot_general x6, matrix products, gather_neighbours(): jnp.einsum('bpw,cbw->cbp', select, window, precision=lax.Precision.HIGHEST)  26.6 us
    ppermute x10, starting transfers between devices, padded_2(): lax.ppermute(head, axis, [((i + 1) % count, i) for i in range(ends)])  22.2 us
    broadcast_in_dim x1, local copies, waits for them, and re-layouts, body(): jnp.broadcast_to(coarse_fix[:, None, :, None, :, None], blocks(shift_diag...  21.4 us
  transfers between devices with their start and end apart: 39, of which 15 were waited for; matrix products, arithmetic and copies ran while one was open for 20% of the time, Pallas kernels for 0%

commit v1 on v0

--- a/solution.py
+++ b/solution.py
@@ -1,7 +1,10 @@
 import jax
 import jax.numpy as jnp
 from jax import lax
+from jax.experimental import pallas as pl
+from jax.experimental.pallas import tpu as pltpu
 from jax.sharding import PartitionSpec as P
+
 
 HALO = 64
 SMOOTH = 3
@@ -119,38 +122,334 @@
     return field.reshape(field.shape[0] // 2, 2, field.shape[1] // 2, 2, field.shape[2] // 2, 2)
 
 
-def gather_neighbours(padded, relative, npoint):
-    block_len = 2 * HALO
-    nblock = npoint // block_len
-    lower = padded[:, :npoint].reshape(3, nblock, block_len)
-    upper = padded[:, block_len:].reshape(3, nblock, block_len)
-    window = jnp.concatenate([lower, upper], axis=2)
-    starts = (jnp.arange(nblock, dtype=jnp.int32) * block_len)[None, :, None]
-    local_idx = relative.reshape(relative.shape[0], nblock, block_len) - starts
-    columns = jnp.arange(2 * block_len, dtype=jnp.int32)
-    picked = []
-    for which in range(relative.shape[0]):
-        select = (local_idx[which][:, :, None] == columns[None, None, :]).astype(jnp.float32)
-        taken = jnp.einsum("bpw,cbw->cbp", select, window, precision=lax.Precision.HIGHEST)
-        picked.append(taken.reshape(3, npoint))
-    return jnp.stack(picked, axis=1)
-
-
-def slot_ranks(owner_ids, ndevice, npoint):
-    block_len = 2 * HALO
-    nblock = npoint // block_len
-    owner_hot = (owner_ids[:, None] == jnp.arange(ndevice, dtype=jnp.int32)[None, :]).astype(
-        jnp.bfloat16
-    )
-    owner_blocks = owner_hot.reshape(nblock, block_len, ndevice)
-    lower_tri = (jnp.arange(block_len)[:, None] > jnp.arange(block_len)[None, :]).astype(
-        jnp.bfloat16
-    )
-    within = jnp.einsum("pq,bqo->bpo", lower_tri, owner_blocks, preferred_element_type=jnp.float32)
-    counts = jnp.sum(owner_blocks.astype(jnp.float32), axis=1)
-    before = jnp.cumsum(counts, axis=0) - counts
-    ranks = jnp.sum((within + before[:, None, :]) * owner_blocks.astype(jnp.float32), axis=2)
-    return (ranks.reshape(npoint).astype(jnp.int32), owner_hot)
+LANES = 128
+BIG = 524288.0
+GROUP_ROWS = 80
+CELL_BITS = 18
+
+
+def permute(value, lane_xor, sub_xor):
+    if sub_xor:
+        where = lax.broadcasted_iota(jnp.int32, value.shape, 0) ^ sub_xor
+        value = pick(value, where, 0)
+    if lane_xor:
+        where = lax.broadcasted_iota(jnp.int32, value.shape, 1) ^ lane_xor
+        value = pick(value, where, 1)
+    return value
+
+
+def pick(value, where, axis):
+    numbers = lax.GatherDimensionNumbers(
+        offset_dims=(),
+        collapsed_slice_dims=(axis,),
+        start_index_map=(axis,),
+        operand_batching_dims=(1 - axis,),
+        start_indices_batching_dims=(1 - axis,),
+    )
+    return lax.gather(
+        value,
+        where[:, :, None],
+        numbers,
+        (1, 1),
+        mode=lax.GatherScatterMode.PROMISE_IN_BOUNDS,
+    )
+
+
+def exchange(keys, loads, places, bits, top):
+    lane_xor = sub_xor = row_xor = 0
+    for bit in bits:
+        kind, amount = places[bit]
+        lane_xor |= amount if kind == "l" else 0
+        sub_xor |= amount if kind == "s" else 0
+        row_xor |= amount if kind == "v" else 0
+    top_kind, top_amount = places[top]
+    count = len(keys)
+    new_keys, new_loads = [None] * count, [None] * count
+    if top_kind == "v":
+        for a in range(count):
+            if a & top_amount:
+                continue
+            b = a ^ row_xor
+            low, high, low_load, high_load = keys[a], keys[b], loads[a], loads[b]
+            stored = b
+            if lane_xor or sub_xor:
+                high = permute(high, lane_xor, sub_xor)
+                high_load = permute(high_load, lane_xor, sub_xor)
+                stored = a | top_amount
+            swap = low > high
+            new_keys[a] = jnp.minimum(low, high)
+            new_keys[stored] = jnp.maximum(low, high)
+            new_loads[a] = jnp.where(swap, high_load, low_load)
+            new_loads[stored] = jnp.where(swap, low_load, high_load)
+        return new_keys, new_loads
+    axis = 1 if top_kind == "l" else 0
+    upper = (lax.broadcasted_iota(jnp.int32, keys[0].shape, axis) & top_amount) != 0
+    for a in range(count):
+        b = a ^ row_xor
+        other = permute(keys[b], lane_xor, sub_xor)
+        other_load = permute(loads[b], lane_xor, sub_xor)
+        best = jnp.where(upper, jnp.maximum(keys[a], other), jnp.minimum(keys[a], other))
+        new_keys[a] = best
+        new_loads[a] = jnp.where(best == keys[a], loads[a], other_load)
+    return new_keys, new_loads
+
+
+def merge_levels(keys, loads, places, first, last):
+    for level in range(first, last + 1):
+        keys, loads = exchange(keys, loads, places, range(level + 1), level)
+        for bit in reversed(range(level)):
+            keys, loads = exchange(keys, loads, places, (bit,), bit)
+    return keys, loads
+
+
+def surface_kernel(
+    begin_ref, low_ref, high_ref, positions_ref, normals_ref, tension_ref, weight_ref,
+    owner_ref, cell_ref, connect_ref, force_ref, packed_ref,
+    wide, jumps, turned, lists, counted, counted_scalar, sem,
+):
+    npoint = positions_ref.shape[1]
+    nrow = npoint // LANES
+    nowner = packed_ref.shape[0]
+    begin, total = begin_ref[0], begin_ref[1]
+    half = lax.broadcasted_iota(jnp.int32, (3, LANES), 1) < HALO
+    before = pltpu.roll(low_ref[...], HALO, 1)
+    for row in range(nrow + 1):
+        source = high_ref[...] if row == nrow else positions_ref[:, row * LANES : (row + 1) * LANES]
+        after = pltpu.roll(source, HALO, 1)
+        wide[0:3, row * LANES : (row + 1) * LANES] = jnp.where(half, before, after)
+        before = after
+
+    def one_row(row, carry):
+        at = pl.multiple_of(row * LANES, LANES)
+        here, there = pl.ds(at, LANES), pl.ds(at + LANES, LANES)
+        blank = jnp.zeros((2, LANES), jnp.int32)
+        index = jnp.concatenate([connect_ref[:, here], blank], axis=0)
+        index = ((index - begin + HALO) & (total - 1)) - at
+        weight = jnp.concatenate([weight_ref[:, here], blank.astype(jnp.float32)], axis=0)
+        second = index >= LANES
+        index = index & (LANES - 1)
+        strength = tension_ref[pl.ds(row, 1), :]
+        jump = jnp.zeros((1, LANES), jnp.float32)
+        for axis in range(3):
+            lower = jnp.broadcast_to(wide[axis : axis + 1, here], (8, LANES))
+            upper = jnp.broadcast_to(wide[axis : axis + 1, there], (8, LANES))
+            taken = jnp.where(second, pick(upper, index, 1), pick(lower, index, 1))
+            pulled = weight * (taken - positions_ref[axis : axis + 1, here])
+            force = strength * jnp.sum(pulled, axis=0, keepdims=True)
+            force_ref[axis : axis + 1, here] = force
+            jump = jump + force * normals_ref[axis : axis + 1, here]
+        jumps[pl.ds(row, 1), :] = jump
+        return carry
+
+    lax.fori_loop(0, nrow, one_row, 0, unroll=8)
+
+    ranks = lax.broadcasted_iota(jnp.int32, (nowner, LANES), 0)
+
+    def count_row(row, below):
+        names = owner_ref[pl.ds(row, 1), :]
+        return below + jnp.where(names < ranks, 1, 0)
+
+    below = lax.fori_loop(0, nrow, count_row, jnp.zeros((nowner, LANES), jnp.int32), unroll=4)
+    starts = jnp.sum(below.astype(jnp.float32), axis=1, keepdims=True)
+    turned[...] = jnp.broadcast_to(starts, (nowner, LANES))
+    counted[...] = jnp.transpose(turned[...])[0:8, :].astype(jnp.int32)
+    fetch = pltpu.make_async_copy(counted, counted_scalar, sem)
+
+    keys, loads = [], []
+    for tile in range(nrow // 8):
+        rows = slice(8 * tile, 8 * tile + 8)
+        cell = cell_ref[rows, :]
+        cell = ((cell & 384) << 9) | ((cell >> 9) << 7) | (cell & 127)
+        keys.append((owner_ref[rows, :] << CELL_BITS) | cell)
+        loads.append(jumps[rows, :])
+    fetch.start()
+    places = [("v", 1), ("v", 2), ("v", 4), ("s", 1), ("s", 2), ("s", 4)]
+    places += [("l", 1 << bit) for bit in range(7)]
+    keys, loads = merge_levels(keys, loads, places, 0, 12)
+    for which, arrays in ((0, keys), (1, loads)):
+        for tile in range(8):
+            value = arrays[tile]
+            if which == 0:
+                value = (value & ((1 << CELL_BITS) - 1)).astype(jnp.float32)
+            turned[pl.ds(tile, 8, stride=8), :] = value
+        flipped = jnp.transpose(turned[...])
+        turned[...] = flipped
+        even = turned[pl.ds(0, 64, stride=2), :]
+        odd = pltpu.roll(turned[pl.ds(1, 64, stride=2), :], 64, 1)
+        lane = lax.broadcasted_iota(jnp.int32, (64, LANES), 1)
+        lists[pl.ds(which, 64, stride=2), :] = jnp.where(lane < 64, even, odd)
+    lists[128:144, :] = jnp.zeros((16, LANES), jnp.float32)
+    fetch.wait()
+
+    lane = lax.broadcasted_iota(jnp.int32, (8, LANES), 1)
+    line = lax.broadcasted_iota(jnp.int32, (8, LANES), 0)
+    slot = lane + LANES * (line >> 1)
+    filler = jnp.where((line & 1) == 0, BIG, 0.0).astype(jnp.float32)
+
+    def one_owner(owner, carry):
+        start = counted_scalar[0, owner]
+        following = jnp.where(owner == nowner - 1, npoint, counted_scalar[0, jnp.minimum(owner + 1, nowner - 1)])
+        shift = start & (LANES - 1)
+        block = lists[pl.ds((start >> 7) * 2, 8), :]
+        block = pltpu.roll(block, (LANES - shift) & (LANES - 1), 1)
+        block = jnp.where(lane < LANES - shift, block, pltpu.roll(block, 6, 0))
+        block = jnp.where(slot < following - start, block, filler)
+        packed_ref[owner] = block[0:4, :]
+        return carry
+
+    lax.fori_loop(0, nowner, one_owner, 0, unroll=8)
+
+
+def spread_kernel(
+    got_ref, rhs_ref, forcing_ref,
+    keys_scratch, loads_scratch, grid, turned, bounds, bounds_scalar, work, sem,
+):
+    nsender = got_ref.shape[0] // 4
+    ngroup = nsender // 32
+    places = [("l", 1 << bit) for bit in range(7)] + [("v", 1), ("v", 2), ("v", 4)]
+    places += [("s", 1), ("s", 2), ("s", 4)]
+
+    def zero(step, carry):
+        grid[pl.ds(pl.multiple_of(step * 64, 64), 64), :] = jnp.zeros((64, LANES), jnp.float32)
+        return carry
+
+    lax.fori_loop(0, grid.shape[0] // 64, zero, 0)
+
+    def one_group(group):
+        keys, loads = [], []
+        for quarter in range(4):
+            for side in range(2):
+                first = (group * 32 + quarter * 8) * 4 + 2 * side
+                keys.append(got_ref[pl.ds(first, 8, stride=4), :])
+                loads.append(got_ref[pl.ds(first + 1, 8, stride=4), :])
+        keys, loads = merge_levels(keys, loads, places, 8, 12)
+        for quarter in range(4):
+            rows = pl.ds(group * 32 + quarter, 8, stride=4)
+            last = jnp.full((8, 1), -1, jnp.int32)
+            base = None
+            for side in range(2):
+                key = keys[2 * quarter + side]
+                columns = slice(side * LANES, (side + 1) * LANES)
+                cell = key.astype(jnp.int32)
+                keys_scratch[side, rows, :] = cell
+                loads_scratch[side, rows, :] = loads[2 * quarter + side]
+                inside = key < BIG
+                line = (cell >> 7).astype(jnp.float32)
+                top = jnp.max(jnp.where(inside, line, -1.0), axis=1, keepdims=True)
+                last = jnp.maximum(last, top.astype(jnp.int32))
+                if side == 0:
+                    base = jnp.min(line, axis=1, keepdims=True).astype(jnp.int32) & -8
+            repeats = jnp.where(last < 0, 0, (((last - base) * 52429) >> 22) + 1)
+            pair = jnp.where(last < 0, 0, base) * 32 + repeats
+            turned[rows, :] = jnp.broadcast_to(pair.astype(jnp.float32), (8, LANES))
+
+    for group in range(ngroup):
+        one_group(group)
+    bounds[...] = jnp.transpose(turned[...])[0:8, :].astype(jnp.int32)
+    fetch = pltpu.make_async_copy(bounds, bounds_scalar, sem)
+    fetch.start()
+    fetch.wait()
+
+    def list_chunk(chunk, filled):
+        pair = bounds_scalar[0, chunk]
+        base = pair >> 5
+
+        def list_piece(piece, filled):
+            work[filled] = (chunk << 12) | (base + piece * GROUP_ROWS)
+            return filled + 1
+
+        return lax.fori_loop(0, pair & 31, list_piece, filled)
+
+    filled = lax.fori_loop(0, 32 * ngroup, list_chunk, 0)
+    for extra in range(BATCH):
+        work[filled + extra] = 2048
+    lines = lax.broadcasted_iota(jnp.int32, (GROUP_ROWS, 2 * LANES), 0)
+    columns = lax.broadcasted_iota(jnp.int32, (LANES, 2 * LANES), 0)
+
+    def one_batch(batch, carry):
+        sums, bases = [], []
+        for piece in range(BATCH):
+            item = work[batch * BATCH + piece]
+            chunk = item >> 12
+            base = pl.multiple_of(item & 4095, 8)
+            cell = jnp.concatenate([keys_scratch[side, pl.ds(chunk, 1), :] for side in range(2)], axis=1)
+            load = jnp.concatenate([loads_scratch[side, pl.ds(chunk, 1), :] for side in range(2)], axis=1)
+            coarse = load.astype(jnp.bfloat16).astype(jnp.float32)
+            here = ((cell >> 7) - base) == lines
+            left = jnp.concatenate(
+                [
+                    jnp.where(here, coarse, 0.0).astype(jnp.bfloat16),
+                    jnp.where(here, load - coarse, 0.0).astype(jnp.bfloat16),
+                ],
+                axis=0,
+            )
+            right = jnp.where((cell & (LANES - 1)) == columns, 1.0, 0.0).astype(jnp.bfloat16)
+            both = lax.dot_general(
+                left, right, (((1,), (1,)), ((), ())), preferred_element_type=jnp.float32
+            )
+            sums.append(both[:GROUP_ROWS] + both[GROUP_ROWS:])
+            bases.append(base)
+        for total, base in zip(sums, bases):
+            grid[pl.ds(base, GROUP_ROWS), :] += total
+        return carry
+
+    lax.fori_loop(0, (filled + BATCH - 1) // BATCH, one_batch, 0)
+
+    shape = forcing_ref.shape
+    for plane in range(shape[0]):
+        for part in range(shape[2] // LANES):
+            columns = slice(part * LANES, (part + 1) * LANES)
+            first = (part * shape[0] + plane) * shape[1]
+            forcing_ref[plane, :, columns] = rhs_ref[plane, :, columns] + grid[first : first + shape[1], :]
+
+
+BATCH = 8
+
+
+def surface_and_pack(begin, low, high, positions, normals, tension, edge_weight, owners, cells, connectivity, nowner):
+    vmem = pl.BlockSpec(memory_space=pltpu.VMEM)
+    return pl.pallas_call(
+        surface_kernel,
+        name="surface",
+        out_shape=(
+            jax.ShapeDtypeStruct(positions.shape, jnp.float32),
+            jax.ShapeDtypeStruct((nowner, 4, LANES), jnp.float32),
+        ),
+        in_specs=[pl.BlockSpec(memory_space=pltpu.SMEM)] + [vmem] * 9,
+        out_specs=(vmem, vmem),
+        scratch_shapes=[
+            pltpu.VMEM((8, positions.shape[1] + LANES), jnp.float32),
+            pltpu.VMEM((positions.shape[1] // LANES, LANES), jnp.float32),
+            pltpu.VMEM((128, LANES), jnp.float32),
+            pltpu.VMEM((144, LANES), jnp.float32),
+            pltpu.VMEM((8, LANES), jnp.int32),
+            pltpu.SMEM((8, LANES), jnp.int32),
+            pltpu.SemaphoreType.DMA,
+        ],
+        compiler_params=pltpu.CompilerParams(vmem_limit_bytes=32 * 1024 * 1024),
+    )(begin, low, high, positions, normals, tension, edge_weight, owners, cells, connectivity)
+
+
+def spread_cells(got, pressure_rhs):
+    vmem = pl.BlockSpec(memory_space=pltpu.VMEM)
+    return pl.pallas_call(
+        spread_kernel,
+        name="spread",
+        out_shape=jax.ShapeDtypeStruct(pressure_rhs.shape, jnp.float32),
+        in_specs=[vmem, vmem],
+        out_specs=vmem,
+        scratch_shapes=[
+            pltpu.VMEM((2, 128, LANES), jnp.int32),
+            pltpu.VMEM((2, 128, LANES), jnp.float32),
+            pltpu.VMEM((2048 + 128, LANES), jnp.float32),
+            pltpu.VMEM((128, LANES), jnp.float32),
+            pltpu.VMEM((8, LANES), jnp.int32),
+            pltpu.SMEM((8, LANES), jnp.int32),
+            pltpu.SMEM((512,), jnp.int32),
+            pltpu.SemaphoreType.DMA,
+        ],
+        compiler_params=pltpu.CompilerParams(vmem_limit_bytes=32 * 1024 * 1024),
+    )(got, pressure_rhs)
 
 
 def body(
@@ -164,35 +463,29 @@
     cell_map,
     connectivity,
 ):
+    every = ("gx", "gy", "gz")
     npoint = positions.shape[1]
-    ndevice = lax.axis_size(("gx", "gy", "gz"))
-    total = npoint * ndevice
-    begin = lax.axis_index(("gx", "gy", "gz")) * npoint
-    padded = padded_2(positions, ((("gx", "gy", "gz"), 1),), HALO, True)
-    relative = (connectivity - begin + HALO + total) % total
-    neighbours = gather_neighbours(padded, relative, npoint)
-    surface_force = tension[None, :] * jnp.sum(
-        edge_weight[None, :, :] * (neighbours - positions[:, None, :]), axis=1
-    )
-    jump = jnp.sum(surface_force * normals, axis=0)
-    owner_ids = owner_map[:, 0]
-    capacity = 4 * npoint // ndevice
-    ranks, owner_hot = slot_ranks(owner_ids, ndevice, npoint)
-    rank_hot = (ranks[:, None] == jnp.arange(capacity, dtype=jnp.int32)[None, :]).astype(
-        jnp.float32
-    )
-    carried = jnp.stack([jump, cell_map.astype(jnp.float32)], axis=0)
-    weighted = carried[:, :, None] * rank_hot[None, :, :]
-    packed = jnp.einsum(
-        "po,kpr->kor", owner_hot.astype(jnp.float32), weighted, precision=lax.Precision.HIGHEST
-    )
-    values = packed[0]
-    cell_ids = packed[1]
-    got_values, got_cells = side_by_side((values, cell_ids), ("gx", "gy", "gz"), 0, 0, 1)
+    ndevice = lax.axis_size(every)
+    begin = lax.axis_index(every) * npoint
+    up = [(i, (i + 1) % ndevice) for i in range(ndevice)]
+    low = lax.ppermute(positions[:, npoint - LANES :], every, up)
+    high = lax.ppermute(positions[:, :LANES], every, [(b, a) for a, b in up])
+    surface_force, packed = surface_and_pack(
+        jnp.stack([begin, npoint * ndevice]).astype(jnp.int32),
+        low,
+        high,
+        positions,
+        normals,
+        tension.reshape(npoint // LANES, LANES),
+        edge_weight,
+        owner_map.reshape(npoint // LANES, LANES),
+        cell_map.reshape(npoint // LANES, LANES),
+        connectivity,
+        ndevice,
+    )
+    got = lax.all_to_all(packed, every, split_axis=0, concat_axis=0, tiled=True)
+    forcing = spread_cells(got.reshape(4 * ndevice, LANES), pressure_rhs)
     shape = pressure_rhs.shape
-    source = jnp.zeros((shape[0] * shape[1] * shape[2],), jnp.float32)
-    source = source.at[got_cells.reshape(-1).astype(jnp.int32)].add(got_values.reshape(-1))
-    forcing = pressure_rhs + source.reshape(shape)
     coarse_shift = 4.0 * jnp.mean(blocks(shift_diag), axis=(1, 3, 5))
     width = SMOOTH
     inside = domain_mask(shape, width)

time: 737 us -> 492 us (0.67)
  other arithmetic: 296 us -> 85.8 us
  matrix products: 37.7 us -> 0 us
  Pallas kernels: 0 us -> 21.4 us
  starting transfers between devices: 130 us -> 116 us
    scatter-add x1 -> x0, other arithmetic: 203 us -> none  [body(): source.at[got_cells.reshape(-1).astype(jnp.int32)]]
    dot_general x8 -> x0, matrix products: 37.7 us -> none  [the longest x6 26.6 us: gather_neighbours(): jnp.einsum('bpw,cbw->cbp', select, window, precision=lax.Precision.HIGHEST)]
    pallas_call x0 -> x2, Pallas kernels: none -> 21.4 us  [the longest x1 13.4 us: spread_cells(): pl.pallas_call(spread_kernel, name='spread', out_shape=jax.ShapeDtypeStru...]
    ppermute x10 -> x9, starting transfers between devices: 50.7 us -> 32.5 us  [padded_2(): lax.ppermute(tail, axis, [(i, (i + 1) % count) for i in range(ends)])]
    unnamed x47 -> x38, local copies, waits for them, and re-layouts: 0.43 us -> 9.02 us
    ppermute x10 -> x9, starting transfers between devices: 22.2 us -> 17.4 us  [padded_2(): lax.ppermute(head, axis, [((i + 1) % count, i) for i in range(ends)])]
    ppermute x10 -> x9, waiting for transfers between devices: 21.1 us -> 20.2 us  [padded_2(): lax.ppermute(head, axis, [((i + 1) % count, i) for i in range(ends)])]
  transfers between devices with their start and end apart: 39 -> 39, of which waited for: 15 -> 15; matrix products, arithmetic and copies ran while one was open for 20% -> 21% of each run, Pallas kernels for 0% -> 2%
where the time goes in v1:
time: 492 us; the launch traced here: 488 us
  local copies, waits for them, and re-layouts  219 us (45%)
  starting transfers between devices  116 us (24%)
  other arithmetic  85.8 us (17%)
  waiting for transfers between devices  44.5 us (9%)
  Pallas kernels  21.4 us (4%)
    reshape x2, local copies, waits for them, and re-layouts, blocks(): field.reshape(field.shape[0] // 2, 2, field.shape[1] // 2, 2, field.shape...  137 us
    reshape x1, local copies, waits for them, and re-layouts, body(): spreadout = jnp.broadcast_to(coarse_fix[:, None, :, None, :, None], block...  47 us
    ppermute x9, starting transfers between devices, extended(): lax.ppermute(last, axis, up)  37 us
    ppermute x9, starting transfers between devices, padded_2(): lax.ppermute(tail, axis, [(i, (i + 1) % count) for i in range(ends)])  32.5 us
    broadcast_in_dim x1, local copies, waits for them, and re-layouts, body(): jnp.broadcast_to(coarse_fix[:, None, :, None, :, None], blocks(shift_diag...  21.4 us
    reduce_sum x1, other arithmetic, body(): coarse_rhs = 0.5 * jnp.sum(blocks(remain), axis=(1, 3, 5))  20.8 us
    reduce_sum x1, other arithmetic, body(): coarse_shift = 4.0 * jnp.mean(blocks(shift_diag), axis=(1, 3, 5))  20.8 us
    ppermute x9, waiting for transfers between devices, padded_2(): lax.ppermute(head, axis, [((i + 1) % count, i) for i in range(ends)])  20.2 us
  transfers between devices with their start and end apart: 39, of which 15 were waited for; matrix products, arithmetic and copies ran while one was open for 21% of the time, Pallas kernels for 2%

profile of v1, /device:TPU:1, one launch (start us, length us, event | category | flops | bytes accessed | tf_op | source)
XLA Modules:
  0.0 488.0 jit_solution(13411989138926775678)
XLA Ops:
  1.3 6.3 %collective-permute-start.7 = (f32[3,128]{1,0:T(4,128)S(1)}, f32[3,128]{1,0:T(4,128)S(1)}, u32[]{:S(2)}, u32[]{:S(2)}) collective-permute-start(f32[3,128]{1,0:T(4,128)S(1)} %get-tuple-element.61), channel_id=1, source_target_pairs={{1,0},{2,1},{3,2},{4,3},{5,4},{6,5},{7,6},{8,7},{9,8},{10,9},{11,1... | collective-permute-start | bytes 4616 | tf_op jit(solution)/shard_map/ppermute | solution.py:472
  8.7 5.3 %collective-permute-start.1 = (f32[3,32,512]{2,1,0:T(8,128)S(1)}, f32[3,32,512]{2,1,0:T(8,128)S(1)}, u32[]{:S(2)}, u32[]{:S(2)}) collective-permute-start(f32[3,32,512]{2,1,0:T(8,128)S(1)} %get-tuple-element.41), channel_id=1, source_target_pairs={{16,0},{32,16},{48,32},{64,48},{80,64},{96,80},{112,96},{17,1},{33... | collective-permute-start | bytes 589832 | tf_op jit(solution)/shard_map/ppermute | solution.py:48
  22.2 8.0 %surface.1 = (f32[3,8192]{1,0:T(4,128)}, f32[128,4,128]{2,1,0:T(4,128)}) custom-call(s32[2]{0:T(128)S(1)} %pad_add_fusion.begin_ref, f32[3,128]{1,0:T(4,128)S(1)} %collective-permute-done.6.low_ref, f32[3,128]{1,0:T(4,128)S(1)} %collective-permute-done.7.high_ref, f32[3,8192]{1,0:T(4,128)S(1)} %copy-done.3, f32[3,8192]{1,0:T(4,128)S(1)} %copy-done.4, ...), custom_call_target="tpu_custom_call" | custom-call | tf_op jit(solution)/shard_map/surface/pallas_call | solution.py:411
  30.2 8.4 %all-to-all-start = ((f32[128,4,128]{2,1,0:T(4,128)}), f32[128,4,128]{2,1,0:T(4,128)S(1)}, u32[]{:S(2)}, u32[]{:S(2)}) async-start(f32[128,4,128]{2,1,0:T(4,128)} %get-tuple-element.4), calls=%async_computation | async-start | bytes 524288 | tf_op jit(solution)/shard_map/all_to_all | solution.py:486
  42.3 7.6 %all-to-all-done = f32[128,4,128]{2,1,0:T(4,128)S(1)} async-done(((f32[128,4,128]{2,1,0:T(4,128)}), f32[128,4,128]{2,1,0:T(4,128)S(1)}, u32[]{:S(2)}, u32[]{:S(2)}) %all-to-all-start) | async-done | bytes 262176 | tf_op jit(solution)/shard_map/all_to_all | solution.py:486
  49.8 13.4 %spread.1 = f32[16,32,512]{2,1,0:T(8,128)S(1)} custom-call(f32[512,128]{1,0:T(8,128)S(1)} %bitcast.7, f32[16,32,512]{2,1,0:T(8,128)S(1)} %copy-done), custom_call_target="tpu_custom_call" | custom-call | tf_op jit(solution)/shard_map/spread/pallas_call | solution.py:435
  73.8 68.4 %reshape.86 = f32[8,2,16,2,256,2]{5,4,3,2,1,0:T(8,128)} reshape(f32[16,32,512]{2,1,0:T(8,128)S(1)} %copy-done.11) | data formatting | bytes 2097152 | tf_op jit(solution)/shard_map/reshape | solution.py:122
  142.1 20.8 %reduce_sum.18 = f32[8,16,256]{2,1,0:T(8,128)S(1)} reduce(f32[8,2,16,2,256,2]{5,4,3,2,1,0:T(8,128)} %reshape.86, f32[]{:T(128)} %constant.16.clone.1), dimensions={1,3,5}, to_apply=%region_0.0 | reduce | flops 229376 | bytes 1179652 | tf_op jit(solution)/shard_map/reduce_sum | solution.py:489
  163.1 4.0 collective-permute-start.10
  169.9 4.4 collective-permute-start.4
  175.9 4.0 collective-permute-start.12
  187.6 4.0 broadcast_divide_fusion
  208.8 68.4 %reshape.87 = f32[8,2,16,2,256,2]{5,4,3,2,1,0:T(8,128)} reshape(f32[16,32,512]{2,1,0:T(8,128)S(1)} %fusion.25) | data formatting | bytes 2097152 | tf_op jit(solution)/shard_map/reshape | solution.py:122
  277.2 20.8 %reduce_sum.19 = f32[8,16,256]{2,1,0:T(8,128)S(1)} reduce(f32[8,2,16,2,256,2]{5,4,3,2,1,0:T(8,128)} %reshape.87, f32[]{:T(128)} %constant.16.clone.1), dimensions={1,3,5}, to_apply=%region_1.2 | reduce | flops 229376 | bytes 1179652 | tf_op jit(solution)/shard_map/reduce_sum | solution.py:499
  309.6 4.0 collective-permute-start.19
  315.6 4.3 collective-permute-start.23
  321.2 4.0 collective-permute-start.21
  328.5 4.6 collective-permute-start.25
  334.7 4.3 collective-permute-start.29
  340.3 4.8 collective-permute-start.27
  348.4 4.8 collective-permute-start.31
  354.5 21.4 %broadcast_in_dim.2 = f32[8,2,16,2,256,2]{5,4,3,2,1,0:T(8,128)} broadcast(f32[8,16,256]{2,1,0:T(8,128)S(1)} %fusion.33), dimensions={0,2,4} | broadcast | bytes 1179648 | tf_op jit(solution)/shard_map/broadcast_in_dim | solution.py:501
  376.0 47.0 %reshape.88 = f32[16,32,512]{2,1,0:T(8,128)S(1)} reshape(f32[8,2,16,2,256,2]{5,4,3,2,1,0:T(8,128)} %broadcast_in_dim.2) | data formatting | bytes 2097152 | tf_op jit(solution)/shard_map/reshape | solution.py:503
  424.8 4.5 collective-permute-start.32
  431.9 4.4 collective-permute-done.33
  436.4 4.3 collective-permute-start.34
  447.2 4.0 collective-permute-start.36
  452.6 6.9 %collective-permute-done.36 = f32[22,38,3]{2,1,0:T(8,128)S(1)} collective-permute-done((f32[22,38,3]{2,1,0:T(8,128)S(1)}, f32[22,38,3]{2,1,0:T(8,128)S(1)}, u32[]{:S(2)}, u32[]{:S(2)}) %collective-permute-start.36) | collective-permute-done | bytes 10064 | tf_op jit(solution)/shard_map/ppermute | solution.py:46
  459.6 4.3 collective-permute-done.37
  467.6 4.5 fusion.68
  472.1 9.2 %add_subtract_fusion = f32[22,38,518]{2,1,0:T(8,128)} fusion(f32[22,38,518]{2,1,0:T(8,128)} %get-tuple-element.8, f32[22,38,518]{2,1,0:T(8,128)S(1)} %get-tuple-element.7), kind=kLoop, calls=%fused_computation.14 | loop fusion | flops 3031336 | bytes 5196576 | tf_op jit(solution)/shard_map/sub | solution.py:72
  481.2 6.7 %slice_add_fusion.1 = f32[16,32,512]{2,1,0:T(8,128)} fusion(f32[22,38,518]{2,1,0:T(8,128)} %get-tuple-element.8, f32[22,38,518]{2,1,0:T(8,128)} %get-tuple-element.9, f32[22,38,518]{2,1,0:T(8,128)} %get-tuple-element.63, f32[22,38,518]{2,1,0:T(8,128)} %get-tuple-element.6, f32[22,38,518]{2,1,0:T(8,128)} %add_subtract_fusion, f32[22,38,518]{2,1,0:T(8,128)S(1)} %copy-done.9), kind=kLoop, calls=%fused_computation.59 | loop fusion | flops 1835008 | bytes 7340032 | tf_op jit(solution)/shard_map/add | solution.py:101
  (139 shorter events, 94.8 us)
Async XLA Ops:
  1.3 14.8 %collective-permute-start.7 = (f32[3,128]{1,0:T(4,128)S(1)}, f32[3,128]{1,0:T(4,128)S(1)}, u32[]{:S(2)}, u32[]{:S(2)}) collective-permute-start(f32[3,128]{1,0:T(4,128)S(1)} %get-tuple-element.61), channel_id=1, source_target_pairs={{1,0},{2,1},{3,2},{4,3},{5,4},{6,5},{7,6},{8,7},{9,8},{10,9},{11,1... | collective-permute-start | bytes 4616 | tf_op jit(solution)/shard_map/ppermute | solution.py:472
  7.6 8.5 %collective-permute-start.6 = (f32[3,128]{1,0:T(4,128)S(1)}, f32[3,128]{1,0:T(4,128)S(1)}, u32[]{:S(2)}, u32[]{:S(2)}) collective-permute-start(f32[3,128]{1,0:T(4,128)S(1)} %get-tuple-element.62), channel_id=1, source_target_pairs={{0,1},{1,2},{2,3},{3,4},{4,5},{5,6},{6,7},{7,8},{8,9},{9,10},{10,1... | collective-permute-start | bytes 4616 | tf_op jit(solution)/shard_map/ppermute | solution.py:471
  8.7 32.9 %collective-permute-start.1 = (f32[3,32,512]{2,1,0:T(8,128)S(1)}, f32[3,32,512]{2,1,0:T(8,128)S(1)}, u32[]{:S(2)}, u32[]{:S(2)}) collective-permute-start(f32[3,32,512]{2,1,0:T(8,128)S(1)} %get-tuple-element.41), channel_id=1, source_target_pairs={{16,0},{32,16},{48,32},{64,48},{80,64},{96,80},{112,96},{17,1},{33... | collective-permute-start | bytes 589832 | tf_op jit(solution)/shard_map/ppermute | solution.py:48
  14.1 24.5 %collective-permute-start = (f32[3,32,512]{2,1,0:T(8,128)S(1)}, f32[3,32,512]{2,1,0:T(8,128)S(1)}, u32[]{:S(2)}, u32[]{:S(2)}) collective-permute-start(f32[3,32,512]{2,1,0:T(8,128)S(1)} %get-tuple-element.42), channel_id=1, source_target_pairs={{0,16},{16,32},{32,48},{48,64},{64,80},{80,96},{96,112},{1,17},{17... | collective-permute-start | bytes 589832 | tf_op jit(solution)/shard_map/ppermute | solution.py:46
  30.2 19.7 %all-to-all-start = ((f32[128,4,128]{2,1,0:T(4,128)}), f32[128,4,128]{2,1,0:T(4,128)S(1)}, u32[]{:S(2)}, u32[]{:S(2)}) async-start(f32[128,4,128]{2,1,0:T(4,128)} %get-tuple-element.4), calls=%async_computation | async-start | bytes 524288 | tf_op jit(solution)/shard_map/all_to_all | solution.py:486
  63.3 99.6 %collective-permute-start.8 = (f32[3,32,512]{2,1,0:T(8,128)S(1)}, f32[3,32,512]{2,1,0:T(8,128)S(1)}, u32[]{:S(2)}, u32[]{:S(2)}) collective-permute-start(f32[3,32,512]{2,1,0:T(8,128)S(1)} %get-tuple-element.39), channel_id=1, source_target_pairs={{0,16},{16,32},{32,48},{48,64},{64,80},{80,96},{96,112},{1,17},{17... | collective-permute-start | bytes 589832 | tf_op jit(solution)/shard_map/ppermute | solution.py:46
  66.3 96.6 %collective-permute-start.9 = (f32[3,32,512]{2,1,0:T(8,128)S(1)}, f32[3,32,512]{2,1,0:T(8,128)S(1)}, u32[]{:S(2)}, u32[]{:S(2)}) collective-permute-start(f32[3,32,512]{2,1,0:T(8,128)S(1)} %get-tuple-element.40), channel_id=1, source_target_pairs={{16,0},{32,16},{48,32},{64,48},{80,64},{96,80},{112,96},{17,1},{33... | collective-permute-start | bytes 589832 | tf_op jit(solution)/shard_map/ppermute | solution.py:48
  70.2 98.2 %collective-permute-start.2 = (f32[22,3,512]{2,1,0:T(4,128)}, f32[22,3,512]{2,1,0:T(4,128)S(1)}, u32[]{:S(2)}, u32[]{:S(2)}) collective-permute-start(f32[22,3,512]{2,1,0:T(4,128)} %get-tuple-element.35), channel_id=1, source_target_pairs={{0,4},{4,8},{8,12},{1,5},{5,9},{9,13},{2,6},{6,10},{10,14},{3,7},{... | collective-permute-start | bytes 405512 | tf_op jit(solution)/shard_map/ppermute | solution.py:46
  72.4 95.9 %collective-permute-start.3 = (f32[22,3,512]{2,1,0:T(4,128)}, f32[22,3,512]{2,1,0:T(4,128)S(1)}, u32[]{:S(2)}, u32[]{:S(2)}) collective-permute-start(f32[22,3,512]{2,1,0:T(4,128)} %get-tuple-element.36), channel_id=1, source_target_pairs={{4,0},{8,4},{12,8},{5,1},{9,5},{13,9},{6,2},{10,6},{14,10},{7,3},{... | collective-permute-start | bytes 405512 | tf_op jit(solution)/shard_map/ppermute | solution.py:48
  163.1 12.6 %collective-permute-start.10 = (f32[22,3,512]{2,1,0:T(4,128)S(1)}, f32[22,3,512]{2,1,0:T(4,128)S(1)}, u32[]{:S(2)}, u32[]{:S(2)}) collective-permute-start(f32[22,3,512]{2,1,0:T(4,128)S(1)} %get-tuple-element.33), channel_id=1, source_target_pairs={{0,4},{4,8},{8,12},{1,5},{5,9},{9,13},{2,6},{6,10},{10,14},{3,7},{... | collective-permute-start | bytes 405512 | tf_op jit(solution)/shard_map/ppermute | solution.py:46
  167.1 8.6 %collective-permute-start.11 = (f32[22,3,512]{2,1,0:T(4,128)S(1)}, f32[22,3,512]{2,1,0:T(4,128)S(1)}, u32[]{:S(2)}, u32[]{:S(2)}) collective-permute-start(f32[22,3,512]{2,1,0:T(4,128)S(1)} %get-tuple-element.34), channel_id=1, source_target_pairs={{4,0},{8,4},{12,8},{5,1},{9,5},{13,9},{6,2},{10,6},{14,10},{7,3},{... | collective-permute-start | bytes 405512 | tf_op jit(solution)/shard_map/ppermute | solution.py:48
  169.9 13.9 %collective-permute-start.4 = (f32[22,38,3]{2,1,0:T(8,128)S(1)}, f32[22,38,3]{2,1,0:T(8,128)S(1)}, u32[]{:S(2)}, u32[]{:S(2)}) collective-permute-start(f32[22,38,3]{2,1,0:T(8,128)S(1)} %get-tuple-element.29), channel_id=1, source_target_pairs={{0,1},{1,2},{2,3},{4,5},{5,6},{6,7},{8,9},{9,10},{10,11},{12,13},{... | collective-permute-start | bytes 30104 | tf_op jit(solution)/shard_map/ppermute | solution.py:46
  174.3 13.3 %collective-permute-start.5 = (f32[22,38,3]{2,1,0:T(8,128)S(1)}, f32[22,38,3]{2,1,0:T(8,128)S(1)}, u32[]{:S(2)}, u32[]{:S(2)}) collective-permute-start(f32[22,38,3]{2,1,0:T(8,128)S(1)} %get-tuple-element.30), channel_id=1, source_target_pairs={{1,0},{2,1},{3,2},{5,4},{6,5},{7,6},{9,8},{10,9},{11,10},{13,12},{... | collective-permute-start | bytes 30104 | tf_op jit(solution)/shard_map/ppermute | solution.py:48
  175.9 17.5 %collective-permute-start.12 = (f32[22,38,3]{2,1,0:T(8,128)S(1)}, f32[22,38,3]{2,1,0:T(8,128)S(1)}, u32[]{:S(2)}, u32[]{:S(2)}) collective-permute-start(f32[22,38,3]{2,1,0:T(8,128)S(1)} %get-tuple-element.27), channel_id=1, source_target_pairs={{0,1},{1,2},{2,3},{4,5},{5,6},{6,7},{8,9},{9,10},{10,11},{12,13},{... | collective-permute-start | bytes 30104 | tf_op jit(solution)/shard_map/ppermute | solution.py:46
  180.0 17.3 %collective-permute-start.13 = (f32[22,38,3]{2,1,0:T(8,128)S(1)}, f32[22,38,3]{2,1,0:T(8,128)S(1)}, u32[]{:S(2)}, u32[]{:S(2)}) collective-permute-start(f32[22,38,3]{2,1,0:T(8,128)S(1)} %get-tuple-element.28), channel_id=1, source_target_pairs={{1,0},{2,1},{3,2},{5,4},{6,5},{7,6},{9,8},{10,9},{11,10},{13,12},{... | collective-permute-start | bytes 30104 | tf_op jit(solution)/shard_map/ppermute | solution.py:48
  298.1 11.5 %collective-permute-start.17 = (f32[8,1,256]{2,1,0:T(1,128)S(1)}, f32[8,1,256]{2,1,0:T(1,128)S(1)}, u32[]{:S(2)}, u32[]{:S(2)}) collective-permute-start(f32[8,1,256]{2,1,0:T(1,128)S(1)} %get-tuple-element.57), channel_id=1, source_target_pairs={{0,4},{4,8},{8,12},{1,5},{5,9},{9,13},{2,6},{6,10},{10,14},{3,7},{... | collective-permute-start | bytes 24584 | tf_op jit(solution)/shard_map/ppermute | solution.py:26
  301.8 11.8 %collective-permute-start.16 = (f32[8,1,256]{2,1,0:T(1,128)S(1)}, f32[8,1,256]{2,1,0:T(1,128)S(1)}, u32[]{:S(2)}, u32[]{:S(2)}) collective-permute-start(f32[8,1,256]{2,1,0:T(1,128)S(1)} %get-tuple-element.58), channel_id=1, source_target_pairs={{4,0},{8,4},{12,8},{5,1},{9,5},{13,9},{6,2},{10,6},{14,10},{7,3},{... | collective-permute-start | bytes 24584 | tf_op jit(solution)/shard_map/ppermute | solution.py:27
  303.1 12.3 %collective-permute-start.15 = (f32[1,16,256]{2,1,0:T(8,128)S(1)}, f32[1,16,256]{2,1,0:T(8,128)S(1)}, u32[]{:S(2)}, u32[]{:S(2)}) collective-permute-start(f32[1,16,256]{2,1,0:T(8,128)S(1)} %get-tuple-element.59), channel_id=1, source_target_pairs={{0,16},{16,32},{32,48},{48,64},{64,80},{80,96},{96,112},{1,17},{17... | collective-permute-start | bytes 49160 | tf_op jit(solution)/shard_map/ppermute | solution.py:26
  305.7 9.7 %collective-permute-start.14 = (f32[1,16,256]{2,1,0:T(8,128)S(1)}, f32[1,16,256]{2,1,0:T(8,128)S(1)}, u32[]{:S(2)}, u32[]{:S(2)}) collective-permute-start(f32[1,16,256]{2,1,0:T(8,128)S(1)} %get-tuple-element.60), channel_id=1, source_target_pairs={{16,0},{32,16},{48,32},{64,48},{80,64},{96,80},{112,96},{17,1},{33... | collective-permute-start | bytes 49160 | tf_op jit(solution)/shard_map/ppermute | solution.py:27
  315.6 12.9 %collective-permute-start.23 = (f32[8,1,256]{2,1,0:T(1,128)S(1)}, f32[8,1,256]{2,1,0:T(1,128)S(1)}, u32[]{:S(2)}, u32[]{:S(2)}) collective-permute-start(f32[8,1,256]{2,1,0:T(1,128)S(1)} %get-tuple-element.51), channel_id=1, source_target_pairs={{0,4},{4,8},{8,12},{1,5},{5,9},{9,13},{2,6},{6,10},{10,14},{3,7},{... | collective-permute-start | bytes 24584 | tf_op jit(solution)/shard_map/ppermute | solution.py:26
  319.9 13.3 %collective-permute-start.22 = (f32[8,1,256]{2,1,0:T(1,128)S(1)}, f32[8,1,256]{2,1,0:T(1,128)S(1)}, u32[]{:S(2)}, u32[]{:S(2)}) collective-permute-start(f32[8,1,256]{2,1,0:T(1,128)S(1)} %get-tuple-element.52), channel_id=1, source_target_pairs={{4,0},{8,4},{12,8},{5,1},{9,5},{13,9},{6,2},{10,6},{14,10},{7,3},{... | collective-permute-start | bytes 24584 | tf_op jit(solution)/shard_map/ppermute | solution.py:27
  321.2 13.3 %collective-permute-start.21 = (f32[1,16,256]{2,1,0:T(8,128)S(1)}, f32[1,16,256]{2,1,0:T(8,128)S(1)}, u32[]{:S(2)}, u32[]{:S(2)}) collective-permute-start(f32[1,16,256]{2,1,0:T(8,128)S(1)} %get-tuple-element.53), channel_id=1, source_target_pairs={{0,16},{16,32},{32,48},{48,64},{64,80},{80,96},{96,112},{1,17},{17... | collective-permute-start | bytes 49160 | tf_op jit(solution)/shard_map/ppermute | solution.py:26
  325.2 9.3 %collective-permute-start.20 = (f32[1,16,256]{2,1,0:T(8,128)S(1)}, f32[1,16,256]{2,1,0:T(8,128)S(1)}, u32[]{:S(2)}, u32[]{:S(2)}) collective-permute-start(f32[1,16,256]{2,1,0:T(8,128)S(1)} %get-tuple-element.54), channel_id=1, source_target_pairs={{16,0},{32,16},{48,32},{64,48},{80,64},{96,80},{112,96},{17,1},{33... | collective-permute-start | bytes 49160 | tf_op jit(solution)/shard_map/ppermute | solution.py:27
  334.7 13.7 %collective-permute-start.29 = (f32[8,1,256]{2,1,0:T(1,128)S(1)}, f32[8,1,256]{2,1,0:T(1,128)S(1)}, u32[]{:S(2)}, u32[]{:S(2)}) collective-permute-start(f32[8,1,256]{2,1,0:T(1,128)S(1)} %get-tuple-element.47), channel_id=1, source_target_pairs={{0,4},{4,8},{8,12},{1,5},{5,9},{9,13},{2,6},{6,10},{10,14},{3,7},{... | collective-permute-start | bytes 24584 | tf_op jit(solution)/shard_map/ppermute | solution.py:26
  339.0 14.3 %collective-permute-start.28 = (f32[8,1,256]{2,1,0:T(1,128)S(1)}, f32[8,1,256]{2,1,0:T(1,128)S(1)}, u32[]{:S(2)}, u32[]{:S(2)}) collective-permute-start(f32[8,1,256]{2,1,0:T(1,128)S(1)} %get-tuple-element.48), channel_id=1, source_target_pairs={{4,0},{8,4},{12,8},{5,1},{9,5},{13,9},{6,2},{10,6},{14,10},{7,3},{... | collective-permute-start | bytes 24584 | tf_op jit(solution)/shard_map/ppermute | solution.py:27
  340.3 14.0 %collective-permute-start.27 = (f32[1,16,256]{2,1,0:T(8,128)S(1)}, f32[1,16,256]{2,1,0:T(8,128)S(1)}, u32[]{:S(2)}, u32[]{:S(2)}) collective-permute-start(f32[1,16,256]{2,1,0:T(8,128)S(1)} %get-tuple-element.45), channel_id=1, source_target_pairs={{0,16},{16,32},{32,48},{48,64},{64,80},{80,96},{96,112},{1,17},{17... | collective-permute-start | bytes 49160 | tf_op jit(solution)/shard_map/ppermute | solution.py:26
  345.1 9.3 %collective-permute-start.26 = (f32[1,16,256]{2,1,0:T(8,128)S(1)}, f32[1,16,256]{2,1,0:T(8,128)S(1)}, u32[]{:S(2)}, u32[]{:S(2)}) collective-permute-start(f32[1,16,256]{2,1,0:T(8,128)S(1)} %get-tuple-element.46), channel_id=1, source_target_pairs={{16,0},{32,16},{48,32},{64,48},{80,64},{96,80},{112,96},{17,1},{33... | collective-permute-start | bytes 49160 | tf_op jit(solution)/shard_map/ppermute | solution.py:27
  424.8 7.1 %collective-permute-start.32 = (f32[3,32,512]{2,1,0:T(8,128)S(1)}, f32[3,32,512]{2,1,0:T(8,128)S(1)}, u32[]{:S(2)}, u32[]{:S(2)}) collective-permute-start(f32[3,32,512]{2,1,0:T(8,128)S(1)} %get-tuple-element.37), channel_id=1, source_target_pairs={{0,16},{16,32},{32,48},{48,64},{64,80},{80,96},{96,112},{1,17},{17... | collective-permute-start | bytes 589832 | tf_op jit(solution)/shard_map/ppermute | solution.py:46
  429.3 7.0 %collective-permute-start.33 = (f32[3,32,512]{2,1,0:T(8,128)S(1)}, f32[3,32,512]{2,1,0:T(8,128)S(1)}, u32[]{:S(2)}, u32[]{:S(2)}) collective-permute-start(f32[3,32,512]{2,1,0:T(8,128)S(1)} %get-tuple-element.38), channel_id=1, source_target_pairs={{16,0},{32,16},{48,32},{64,48},{80,64},{96,80},{112,96},{17,1},{33... | collective-permute-start | bytes 589832 | tf_op jit(solution)/shard_map/ppermute | solution.py:48
  436.4 6.7 %collective-permute-start.34 = (f32[22,3,512]{2,1,0:T(4,128)S(1)}, f32[22,3,512]{2,1,0:T(4,128)S(1)}, u32[]{:S(2)}, u32[]{:S(2)}) collective-permute-start(f32[22,3,512]{2,1,0:T(4,128)S(1)} %get-tuple-element.31), channel_id=1, source_target_pairs={{0,4},{4,8},{8,12},{1,5},{5,9},{9,13},{2,6},{6,10},{10,14},{3,7},{... | collective-permute-start | bytes 405512 | tf_op jit(solution)/shard_map/ppermute | solution.py:46
  447.2 12.4 %collective-permute-start.36 = (f32[22,38,3]{2,1,0:T(8,128)S(1)}, f32[22,38,3]{2,1,0:T(8,128)S(1)}, u32[]{:S(2)}, u32[]{:S(2)}) collective-permute-start(f32[22,38,3]{2,1,0:T(8,128)S(1)} %get-tuple-element.25), channel_id=1, source_target_pairs={{0,1},{1,2},{2,3},{4,5},{5,6},{6,7},{8,9},{9,10},{10,11},{12,13},{... | collective-permute-start | bytes 30104 | tf_op jit(solution)/shard_map/ppermute | solution.py:46
  451.2 12.6 %collective-permute-start.37 = (f32[22,38,3]{2,1,0:T(8,128)S(1)}, f32[22,38,3]{2,1,0:T(8,128)S(1)}, u32[]{:S(2)}, u32[]{:S(2)}) collective-permute-start(f32[22,38,3]{2,1,0:T(8,128)S(1)} %get-tuple-element.26), channel_id=1, source_target_pairs={{1,0},{2,1},{3,2},{5,4},{6,5},{7,6},{9,8},{10,9},{11,10},{13,12},{... | collective-permute-start | bytes 30104 | tf_op jit(solution)/shard_map/ppermute | solution.py:48
  (25 other events, 219.2 us)

commit v2 on v1

--- a/solution.py
+++ b/solution.py
@@ -1,3 +1,4 @@
+import functools
 import jax
 import jax.numpy as jnp
 from jax import lax
@@ -5,7 +6,6 @@
 from jax.experimental.pallas import tpu as pltpu
 from jax.sharding import PartitionSpec as P
 
-
 HALO = 64
 SMOOTH = 3
 COARSE_SMOOTH = 4
@@ -13,113 +13,6 @@
 
 centre = 1.125
 spread = 0.875
-
-
-def extended(value, sides, width):
-    edges = {}
-    for axis, dim in sides:
-        devices, length = (lax.axis_size(axis), value.shape[dim])
-        up = [(i, (i + 1) % devices) for i in range(devices - 1)]
-        last = lax.slice_in_dim(value, length - width, length, axis=dim)
-        initial = lax.slice_in_dim(value, 0, width, axis=dim)
-        edges[dim] = (
-            lax.ppermute(last, axis, up),
-            lax.ppermute(initial, axis, [(b, a) for a, b in up]),
-        )
-    done = []
-    for _, dim in sides:
-        low, high = edges[dim]
-        around = [(width, width) if d in done else (0, 0) for d in range(value.ndim)]
-        value = jnp.concatenate([jnp.pad(low, around), value, jnp.pad(high, around)], axis=dim)
-        done.append(dim)
-    return value
-
-
-def padded_2(cells, sides, width, closed):
-    for axis, dim in sides:
-        count = lax.axis_size(axis)
-        ends = count if closed else count - 1
-        head = lax.slice_in_dim(cells, 0, width, axis=dim)
-        tail = lax.slice_in_dim(cells, cells.shape[dim] - width, cells.shape[dim], axis=dim)
-        cells = jnp.concatenate(
-            [
-                lax.ppermute(tail, axis, [(i, (i + 1) % count) for i in range(ends)]),
-                cells,
-                lax.ppermute(head, axis, [((i + 1) % count, i) for i in range(ends)]),
-            ],
-            axis=dim,
-        )
-    return cells
-
-
-def side_by_side(arrays, axis, split_dim, concat_dim, along):
-    both = jnp.concatenate(arrays, axis=along)
-    filled, at, outs = (
-        lax.all_to_all(both, axis, split_axis=split_dim, concat_axis=concat_dim, tiled=True),
-        0,
-        [],
-    )
-    for a in arrays:
-        outs.append(lax.slice_in_dim(filled, at, at + a.shape[along], axis=along))
-        at += a.shape[along]
-    return tuple(outs)
-
-
-def stencil(padded, field, shift):
-    beside = padded[2:, 1:-1, 1:-1] + padded[:-2, 1:-1, 1:-1]
-    beside = beside + padded[1:-1, 2:, 1:-1] + padded[1:-1, :-2, 1:-1]
-    beside = beside + padded[1:-1, 1:-1, 2:] + padded[1:-1, 1:-1, :-2]
-    return (6.0 + shift) * field - beside
-
-
-def coarse_apply(field, shift):
-    padded = extended(field, (("gx", 0), ("gy", 1), ("gz", 2)), 1)
-    return stencil(padded, field, shift)
-
-
-def local_apply(field, shift):
-    return stencil(jnp.pad(field, 1), field, shift)
-
-
-def chebyshev(target, shift, start, sweeps, apply_fn, inside):
-    inverse = 1.0 / (6.0 + shift)
-    ratio = centre / spread
-    factor = 1.0 / ratio
-    if start is None:
-        update = inverse * target / centre
-        answer = update
-    else:
-        update = inverse * (target - apply_fn(start, shift)) / centre
-        update = update * inside
-        answer = start + update
-    for sweep in range(1, sweeps):
-        remain = inverse * (target - apply_fn(answer, shift))
-        if inside is not None:
-            remain = remain * inside
-        factor_new = 1.0 / (2.0 * ratio - factor)
-        update = factor_new * factor * update + 2.0 * factor_new / spread * remain
-        answer = answer + update
-        factor = factor_new
-    return answer
-
-
-def domain_mask(shape, width):
-    places = (lax.axis_index("gx"), lax.axis_index("gy"), lax.axis_index("gz"))
-    counts = (lax.axis_size("gx"), lax.axis_size("gy"), lax.axis_size("gz"))
-    factors = []
-    for which in range(3):
-        length = shape[which]
-        where = places[which] * length - width + jnp.arange(length + 2 * width, dtype=jnp.int32)
-        factors.append(((where >= 0) & (where < length * counts[which])).astype(jnp.float32))
-    return factors[0][:, None, None] * factors[1][None, :, None] * factors[2][None, None, :]
-
-
-def interior(field, width):
-    return field[width:-width, width:-width, width:-width]
-
-
-def blocks(field):
-    return field.reshape(field.shape[0] // 2, 2, field.shape[1] // 2, 2, field.shape[2] // 2, 2)
 
 
 LANES = 128
@@ -452,6 +345,284 @@
     )(got, pressure_rhs)
 
 
+AXES = ("gx", "gy", "gz")
+
+
+def halo_copies(sides, slot, send_sems, recv_sems):
+    copies = []
+    for which, (axis, step, source, target) in enumerate(sides):
+        here = lax.axis_index(axis)
+        there = here + step
+        back = here - step
+        size = lax.axis_size(axis)
+        copy = pltpu.make_async_remote_copy(
+            src_ref=source,
+            dst_ref=target,
+            send_sem=send_sems.at[slot, which],
+            recv_sem=recv_sems.at[slot, which],
+            device_id={axis: there},
+            device_id_type=pl.DeviceIdType.MESH,
+        )
+        copies.append((copy, (there >= 0) & (there < size), (back >= 0) & (back < size)))
+    return copies
+
+
+def cycle_kernel(
+    plane_rows, forcing_ref, shift_ref, pressure_ref,
+    wide_a, wide_b, coarse_a, coarse_b, inverse, update, coarse_rhs, coarse_inverse, coarse_update,
+    rows_out, rows_in, columns_out, columns_in, send_sems, recv_sems,
+):
+    width = forcing_ref.shape[1]
+    nplane = forcing_ref.shape[0] // plane_rows
+    ncoarse = nplane // 2
+    tiles = plane_rows // 8
+    wide, coarse = (wide_a, wide_b), (coarse_a, coarse_b)
+    blank = jnp.zeros((plane_rows, width), jnp.float32)
+    for slot in range(2):
+        wide[slot][0:plane_rows, :] = blank
+        wide[slot][(nplane + 1) * plane_rows : (nplane + 2) * plane_rows, :] = blank
+        coarse[slot][0:plane_rows, :] = blank
+        coarse[slot][(ncoarse + 1) * plane_rows : (ncoarse + 2) * plane_rows, :] = blank
+        for side in range(2):
+            rows_in[slot, side] = jnp.zeros(rows_in.shape[2:], jnp.float32)
+            columns_in[slot, side] = jnp.zeros(columns_in.shape[2:], jnp.float32)
+
+    barrier = pltpu.get_barrier_semaphore()
+    neighbours = 0
+    for axis in AXES:
+        here, size = lax.axis_index(axis), lax.axis_size(axis)
+        for step in (-1, 1):
+            there = here + step
+            exists = (there >= 0) & (there < size)
+            neighbours = neighbours + exists.astype(jnp.int32)
+
+            @pl.when(exists)
+            def _():
+                pl.semaphore_signal(
+                    barrier, inc=1, device_id={axis: there}, device_id_type=pl.DeviceIdType.MESH
+                )
+
+    pl.semaphore_wait(barrier, neighbours)
+
+    lane = lax.broadcasted_iota(jnp.int32, (8, LANES), 1)
+
+    def columns_of(field, plane, slot, low, high):
+        rows_out[slot, 0, pl.ds(plane, 1), :] = field[0:1, :]
+        rows_out[slot, 1, pl.ds(plane, 1), :] = field[plane_rows - 1 : plane_rows, :]
+        for tile in range(tiles):
+            rows = slice(8 * tile, 8 * tile + 8)
+            mine = lane == plane * tiles + tile
+            first = pick(field[rows, 0:LANES], jnp.zeros((8, LANES), jnp.int32), 1)
+            last = pick(field[rows, width - LANES : width], jnp.full((8, LANES), LANES - 1, jnp.int32), 1)
+            low = jnp.where(mine, first, low)
+            high = jnp.where(mine, last, high)
+        return low, high
+
+    def exchange_faces(field, count, slot, low, high):
+        columns_out[slot, 0] = low
+        columns_out[slot, 1] = high
+        here = pl.ds(0, count)
+
+        def planes(first):
+            return field.at[pl.ds(first * plane_rows, plane_rows), :]
+
+        sides = (
+            ("gx", -1, planes(1), planes(count + 1)),
+            ("gx", 1, planes(count), planes(0)),
+            ("gy", -1, rows_out.at[slot, 0, here], rows_in.at[slot, 1, here]),
+            ("gy", 1, rows_out.at[slot, 1, here], rows_in.at[slot, 0, here]),
+            ("gz", -1, columns_out.at[slot, 0], columns_in.at[slot, 1]),
+            ("gz", 1, columns_out.at[slot, 1], columns_in.at[slot, 0]),
+        )
+        copies = halo_copies(sides, slot, send_sems, recv_sems)
+        for copy, sends, receives in copies:
+            pl.when(sends)(copy.start)
+        for copy, sends, receives in copies:
+            pl.when(sends)(copy.wait_send)
+            pl.when(receives)(copy.wait_recv)
+
+    row_index = lax.broadcasted_iota(jnp.int32, (plane_rows, width), 0)
+    lane_index = lax.broadcasted_iota(jnp.int32, (plane_rows, LANES), 1)
+
+    def beside(field, plane, slot, reach):
+        first = pl.multiple_of((plane + 1) * plane_rows, plane_rows)
+        centre_plane = field[pl.ds(first, plane_rows), :]
+        total = field[pl.ds(first - plane_rows, plane_rows), :] + field[pl.ds(first + plane_rows, plane_rows), :]
+        above = rows_in[slot, 0, pl.ds(plane, 1), :]
+        below = rows_in[slot, 1, pl.ds(plane, 1), :]
+        total = total + jnp.where(row_index < reach, above, pltpu.roll(centre_plane, reach, 0))
+        total = total + jnp.where(
+            row_index >= plane_rows - reach, below, pltpu.roll(centre_plane, plane_rows - reach, 0)
+        )
+        spread_low, spread_high = [], []
+        for tile in range(tiles):
+            where = jnp.full((8, LANES), plane * tiles + tile, jnp.int32)
+            spread_low.append(pick(columns_in[slot, 0], where, 1))
+            spread_high.append(pick(columns_in[slot, 1], where, 1))
+        left = pltpu.roll(centre_plane, reach, 1)
+        right = pltpu.roll(centre_plane, width - reach, 1)
+        left_edge = jnp.where(lane_index < reach, jnp.concatenate(spread_low, axis=0), left[:, :LANES])
+        right_edge = jnp.where(
+            lane_index >= LANES - reach, jnp.concatenate(spread_high, axis=0), right[:, width - LANES :]
+        )
+        total = total + jnp.concatenate([left_edge, left[:, LANES:]], axis=1)
+        total = total + jnp.concatenate([right[:, : width - LANES], right_edge], axis=1)
+        return centre_plane, total
+
+    def rows_of(plane):
+        return pl.ds(pl.multiple_of(plane * plane_rows, plane_rows), plane_rows)
+
+    nothing = jnp.zeros((8, LANES), jnp.float32)
+
+    def each_plane(count, step):
+        return lax.fori_loop(0, count, step, (nothing, nothing))
+
+    def sweep(source, target, slot, count, reach, rhs, scale, change, keep, gain, out=None):
+        def step(plane, carry):
+            here = rows_of(plane)
+            field, total = beside(source, plane, slot, reach)
+            remain = scale[here, :] * (rhs[here, :] + total) - field
+            moved = gain * remain
+            if keep:
+                moved = moved + keep * change[here, :]
+            answer = field + moved
+            if out is not None:
+                out[here, :] = answer
+                return carry
+            change[here, :] = moved
+            target[rows_of(plane + 1), :] = answer
+            return columns_of(answer, plane, 1 - slot, *carry)
+
+        return each_plane(count, step)
+
+    ratio = centre / spread
+    gains, factor = [], 1.0 / ratio
+    for _ in range(COARSE_SMOOTH):
+        factor_new = 1.0 / (2.0 * ratio - factor)
+        gains.append((factor_new * factor, 2.0 * factor_new / spread))
+        factor = factor_new
+
+    def first_step(plane, carry):
+        here = rows_of(plane)
+        scale = 1.0 / (6.0 + shift_ref[here, :])
+        inverse[here, :] = scale
+        answer = scale * forcing_ref[here, :] * (1.0 / centre)
+        update[here, :] = answer
+        wide_a[rows_of(plane + 1), :] = answer
+        return columns_of(answer, plane, 0, *carry)
+
+    edges = each_plane(nplane, first_step)
+    slot = 0
+    exchange_faces(wide[slot], nplane, slot, *edges)
+    for sweep_index in range(SMOOTH - 1):
+        keep, gain = gains[sweep_index]
+        edges = sweep(
+            wide[slot], wide[1 - slot], slot, nplane, 1, forcing_ref, inverse, update, keep, gain
+        )
+        slot = 1 - slot
+        exchange_faces(wide[slot], nplane, slot, *edges)
+    smooth = wide[slot]
+
+    lane_pair = lax.broadcasted_iota(jnp.int32, (8, LANES), 1) ^ 1
+    line_pair = lax.broadcasted_iota(jnp.int32, (8, LANES), 0) ^ 1
+
+    def pair_sum(value):
+        lines = []
+        for tile in range(tiles):
+            parts = []
+            for part in range(width // LANES):
+                block = value[8 * tile : 8 * tile + 8, part * LANES : (part + 1) * LANES]
+                block = block + pick(block, lane_pair, 1)
+                parts.append(block + pick(block, line_pair, 0))
+            lines.append(jnp.concatenate(parts, axis=1))
+        return jnp.concatenate(lines, axis=0)
+
+    smooth_slot = slot
+    slot = 1 - slot
+
+    def restrict(plane, carry):
+        remains, shifts = None, None
+        for half in range(2):
+            fine = 2 * plane + half
+            here = rows_of(fine)
+            field, total = beside(smooth, fine, smooth_slot, 1)
+            shift = shift_ref[here, :]
+            remain = forcing_ref[here, :] - ((6.0 + shift) * field - total)
+            remains = remain if remains is None else remains + remain
+            shifts = shift if shifts is None else shifts + shift
+        rhs = 0.5 * pair_sum(remains)
+        scale = 1.0 / (6.0 + 0.5 * pair_sum(shifts))
+        answer = scale * rhs * (1.0 / centre)
+        here = rows_of(plane)
+        coarse_rhs[here, :] = rhs
+        coarse_inverse[here, :] = scale
+        coarse_update[here, :] = answer
+        coarse[slot][rows_of(plane + 1), :] = answer
+        return columns_of(answer, plane, slot, *carry)
+
+    edges = each_plane(ncoarse, restrict)
+    for sweep_index in range(COARSE_SMOOTH - 1):
+        exchange_faces(coarse[slot], ncoarse, slot, *edges)
+        keep, gain = gains[sweep_index]
+        edges = sweep(
+            coarse[slot], coarse[1 - slot], slot, ncoarse, 2,
+            coarse_rhs, coarse_inverse, coarse_update, keep, gain,
+        )
+        slot = 1 - slot
+    fix = coarse[slot]
+
+    def begin_again(plane, carry):
+        here = rows_of(plane + 1)
+        answer = smooth[here, :] + fix[rows_of(lax.div(plane, 2) + 1), :]
+        wide[slot][here, :] = answer
+        return columns_of(answer, plane, slot, *carry)
+
+    edges = each_plane(nplane, begin_again)
+    for sweep_index in range(SMOOTH):
+        exchange_faces(wide[slot], nplane, slot, *edges)
+        keep, gain = gains[sweep_index - 1] if sweep_index else (0.0, 1.0 / centre)
+        edges = sweep(
+            wide[slot], wide[1 - slot], slot, nplane, 1, forcing_ref, inverse, update, keep, gain,
+            pressure_ref if sweep_index == SMOOTH - 1 else None,
+        )
+        slot = 1 - slot
+
+
+def multigrid(forcing, shift_diag):
+    planes, rows, width = forcing.shape
+    vmem = pl.BlockSpec(memory_space=pltpu.VMEM)
+    flat = (planes * rows, width)
+    half = (planes // 2 * rows, width)
+    f32 = jnp.float32
+    return pl.pallas_call(
+        functools.partial(cycle_kernel, rows),
+        name="multigrid",
+        out_shape=jax.ShapeDtypeStruct(flat, f32),
+        in_specs=[vmem, vmem],
+        out_specs=vmem,
+        scratch_shapes=[
+            pltpu.VMEM((flat[0] + 2 * rows, width), f32),
+            pltpu.VMEM((flat[0] + 2 * rows, width), f32),
+            pltpu.VMEM((half[0] + 2 * rows, width), f32),
+            pltpu.VMEM((half[0] + 2 * rows, width), f32),
+            pltpu.VMEM(flat, f32),
+            pltpu.VMEM(flat, f32),
+            pltpu.VMEM(half, f32),
+            pltpu.VMEM(half, f32),
+            pltpu.VMEM(half, f32),
+            pltpu.VMEM((2, 2, planes, width), f32),
+            pltpu.VMEM((2, 2, planes, width), f32),
+            pltpu.VMEM((2, 2, 8, LANES), f32),
+            pltpu.VMEM((2, 2, 8, LANES), f32),
+            pltpu.SemaphoreType.DMA((2, 6)),
+            pltpu.SemaphoreType.DMA((2, 6)),
+        ],
+        compiler_params=pltpu.CompilerParams(
+            vmem_limit_bytes=48 * 1024 * 1024, collective_id=0, has_side_effects=True
+        ),
+    )(forcing.reshape(flat), shift_diag.reshape(flat)).reshape(forcing.shape)
+
+
 def body(
     pressure_rhs,
     shift_diag,
@@ -485,26 +656,7 @@
     )
     got = lax.all_to_all(packed, every, split_axis=0, concat_axis=0, tiled=True)
     forcing = spread_cells(got.reshape(4 * ndevice, LANES), pressure_rhs)
-    shape = pressure_rhs.shape
-    coarse_shift = 4.0 * jnp.mean(blocks(shift_diag), axis=(1, 3, 5))
-    width = SMOOTH
-    inside = domain_mask(shape, width)
-    forcing_wide, shift_wide = (
-        padded_2(forcing, (("gx", 0), ("gy", 1), ("gz", 2)), width, False),
-        padded_2(shift_diag, (("gx", 0), ("gy", 1), ("gz", 2)), width, False),
-    )
-    smooth_wide = chebyshev(forcing_wide, shift_wide, None, SMOOTH, local_apply, inside)
-    remain = interior(forcing_wide - local_apply(smooth_wide, shift_wide), width)
-    smooth = interior(smooth_wide, width)
-    coarse_rhs = 0.5 * jnp.sum(blocks(remain), axis=(1, 3, 5))
-    coarse_fix = chebyshev(coarse_rhs, coarse_shift, None, COARSE_SMOOTH, coarse_apply, None)
-    spreadout = jnp.broadcast_to(
-        coarse_fix[:, None, :, None, :, None], blocks(shift_diag).shape
-    ).reshape(shape)
-    start_wide = padded_2(smooth + spreadout, (("gx", 0), ("gy", 1), ("gz", 2)), width, False)
-    pressure = interior(
-        chebyshev(forcing_wide, shift_wide, start_wide, SMOOTH, local_apply, inside), width
-    )
+    pressure = multigrid(forcing, shift_diag)
     return (pressure, surface_force)
 
 

time: 492 us -> 115 us (0.23)
  local copies, waits for them, and re-layouts: 219 us -> 7.75 us
  starting transfers between devices: 116 us -> 6.31 us
  other arithmetic: 85.8 us -> 0.07 us
  Pallas kernels: 21.4 us -> 73.4 us
  waiting for transfers between devices: 44.5 us -> 6.25 us
  blocking collectives: 0 us -> 19.6 us
    reshape x3 -> x0, local copies, waits for them, and re-layouts: 184 us -> none  [the longest x2 137 us: blocks(): field.reshape(field.shape[0] // 2, 2, field.shape[1] // 2, 2, field.shape...]
    ppermute x36 -> x0, starting transfers between devices: 101 us -> none  [the longest x9 37 us: extended(): lax.ppermute(last, axis, up)]
    pallas_call x0 -> x1, Pallas kernels: none -> 52.2 us  [multigrid(): pl.pallas_call(functools.partial(cycle_kernel, rows), name='multigrid', o...]
    reduce_sum x2 -> x0, other arithmetic: 41.6 us -> none  [the longest x1 20.8 us: body(): coarse_rhs = 0.5 * jnp.sum(blocks(remain), axis=(1, 3, 5))]
    ppermute x36 -> x0, waiting for transfers between devices: 37 us -> none  [the longest x9 20.2 us: padded_2(): lax.ppermute(head, axis, [((i + 1) % count, i) for i in range(ends)])]
    add x10 -> x0, other arithmetic: 23.6 us -> none  [the longest x7 17.3 us: chebyshev(): answer = answer + update]
    broadcast_in_dim x1 -> x0, local copies, waits for them, and re-layouts: 21.4 us -> none  [body(): jnp.broadcast_to(coarse_fix[:, None, :, None, :, None], blocks(shift_diag...]
    all_to_all x0 -> x1, blocking collectives: none -> 19.6 us  [body(): got = lax.all_to_all(packed, every, split_axis=0, concat_axis=0, tiled=True)]
  transfers between devices with their start and end apart: 39 -> 2, of which waited for: 15 -> 2; matrix products, arithmetic and copies ran while one was open for 21% -> 0% of each run, Pallas kernels for 2% -> 0%
where the time goes in v2:
time: 115 us; the launch traced here: 114 us
  Pallas kernels  73.4 us (64%)
  blocking collectives  19.6 us (17%)
  local copies, waits for them, and re-layouts  7.75 us (7%)
  starting transfers between devices  6.31 us (5%)
  waiting for transfers between devices  6.25 us (5%)
    pallas_call x1, Pallas kernels, multigrid(): pl.pallas_call(functools.partial(cycle_kernel, rows), name='multigrid', o...  52.2 us
    all_to_all x1, blocking collectives, body(): got = lax.all_to_all(packed, every, split_axis=0, concat_axis=0, tiled=True)  19.6 us
    pallas_call x1, Pallas kernels, spread_cells(): pl.pallas_call(spread_kernel, name='spread', out_shape=jax.ShapeDtypeStru...  13.4 us
    pallas_call x1, Pallas kernels, surface_and_pack(): pl.pallas_call(surface_kernel, name='surface', out_shape=(jax.ShapeDtypeS...  7.87 us
    unnamed x19, local copies, waits for them, and re-layouts  6.96 us
    ppermute x1, starting transfers between devices, body(): high = lax.ppermute(positions[:, :LANES], every, [(b, a) for a, b in up])  6.31 us
    ppermute x1, waiting for transfers between devices, body(): low = lax.ppermute(positions[:, npoint - LANES:], every, up)  5.59 us
  transfers between devices with their start and end apart: 2, of which 2 were waited for; matrix products, arithmetic and copies ran while one was open for 0% of the time, Pallas kernels for 0%

profile of v2, /device:TPU:1, one launch (start us, length us, event | category | flops | bytes accessed | tf_op | source)
XLA Modules:
  0.0 114.1 jit_solution(10233740535227457391)
XLA Ops:
  0.6 0.0 copy-start.1
  0.6 0.8 fusion
  1.4 6.3 %collective-permute-start.1 = (f32[3,128]{1,0:T(4,128)S(1)}, f32[3,128]{1,0:T(4,128)S(1)}, u32[]{:S(2)}, u32[]{:S(2)}) collective-permute-start(f32[3,128]{1,0:T(4,128)S(1)} %get-tuple-element.6), channel_id=1, source_target_pairs={{1,0},{2,1},{3,2},{4,3},{5,4},{6,5},{7,6},{8,7},{9,8},{10,9},{11,1... | collective-permute-start | bytes 4616 | tf_op jit(solution)/shard_map/ppermute | solution.py:643
  7.7 0.0 collective-permute-start
  7.7 0.1 pad_add_fusion.begin_ref
  7.8 0.7 collective-permute-done.1.high_ref
  8.5 5.6 %collective-permute-done.low_ref = f32[3,128]{1,0:T(4,128)S(1)} collective-permute-done((f32[3,128]{1,0:T(4,128)S(1)}, f32[3,128]{1,0:T(4,128)S(1)}, u32[]{:S(2)}, u32[]{:S(2)}) %collective-permute-start) | collective-permute-done | bytes 1568 | tf_op jit(solution)/shard_map/ppermute | solution.py:642
  14.1 0.0 copy-start.2
  14.1 0.9 copy-done.2
  15.0 0.0 copy-start.3
  15.0 0.9 copy-done.3
  16.0 0.0 copy-start.4
  16.0 0.9 copy-done.4
  16.9 0.0 copy-start.5
  16.9 0.9 copy-done.5
  17.8 0.0 copy-start.6
  17.8 0.8 copy-done.6
  18.5 0.0 copy-start.7
  18.5 0.8 copy-done.7
  19.3 0.0 copy-start.8
  19.3 0.8 copy-done.8
  20.1 7.9 %surface.1 = (f32[3,8192]{1,0:T(4,128)}, f32[128,4,128]{2,1,0:T(4,128)S(1)}) custom-call(s32[2]{0:T(128)S(1)} %pad_add_fusion.begin_ref, f32[3,128]{1,0:T(4,128)S(1)} %collective-permute-done.low_ref, f32[3,128]{1,0:T(4,128)S(1)} %collective-permute-done.1.high_ref, f32[3,8192]{1,0:T(4,128)S(1)} %copy-done.4, f32[3,8192]{1,0:T(4,128)S(1)} %copy-done.5, ...), custom_call_target="tpu_custom_call" | custom-call | tf_op jit(solution)/shard_map/surface/pallas_call | solution.py:304
  27.9 19.6 %all_to_all.5 = f32[128,4,128]{2,1,0:T(4,128)S(1)} all-to-all(f32[128,4,128]{2,1,0:T(4,128)S(1)} %get-tuple-element.4), channel_id=1, replica_groups=mesh['gx'=8,'gy'=4,'gz'=4] {'gx','gy','gz'}, dimensions={0} | all-to-all | bytes 524288 | tf_op jit(solution)/shard_map/all_to_all | solution.py:657
  47.5 0.0 copy-done.1
  47.5 0.0 copy-start
  47.5 13.4 %spread.1 = f32[16,32,512]{2,1,0:T(8,128)S(1)} custom-call(f32[512,128]{1,0:T(8,128)S(1)} %bitcast.11, f32[16,32,512]{2,1,0:T(8,128)S(1)} %copy-done.1), custom_call_target="tpu_custom_call" | custom-call | tf_op jit(solution)/shard_map/spread/pallas_call | solution.py:328
  60.9 0.0 copy-done
  60.9 52.2 %multigrid.1 = f32[512,512]{1,0:T(8,128)S(1)} custom-call(f32[512,512]{1,0:T(8,128)S(1)} %bitcast.9, f32[512,512]{1,0:T(8,128)S(1)} %bitcast.10), custom_call_target="tpu_custom_call" | custom-call | tf_op jit(solution)/shard_map/multigrid/pallas_call | solution.py:597
  113.1 1.0 copy.12
Async XLA Ops:
  0.6 46.9 %copy-start.1 = (f32[16,32,512]{2,1,0:T(8,128)S(1)}, f32[16,32,512]{2,1,0:T(8,128)}, u32[]{:S(2)}) copy-start(f32[16,32,512]{2,1,0:T(8,128)} %rhs_ref.1) | copy-start | bytes 3145732
  1.4 7.0 %collective-permute-start.1 = (f32[3,128]{1,0:T(4,128)S(1)}, f32[3,128]{1,0:T(4,128)S(1)}, u32[]{:S(2)}, u32[]{:S(2)}) collective-permute-start(f32[3,128]{1,0:T(4,128)S(1)} %get-tuple-element.6), channel_id=1, source_target_pairs={{1,0},{2,1},{3,2},{4,3},{5,4},{6,5},{7,6},{8,7},{9,8},{10,9},{11,1... | collective-permute-start | bytes 4616 | tf_op jit(solution)/shard_map/ppermute | solution.py:643
  7.7 6.3 %collective-permute-start = (f32[3,128]{1,0:T(4,128)S(1)}, f32[3,128]{1,0:T(4,128)S(1)}, u32[]{:S(2)}, u32[]{:S(2)}) collective-permute-start(f32[3,128]{1,0:T(4,128)S(1)} %get-tuple-element.7), channel_id=1, source_target_pairs={{0,1},{1,2},{2,3},{3,4},{4,5},{5,6},{6,7},{7,8},{8,9},{9,10},{10,1... | collective-permute-start | bytes 4616 | tf_op jit(solution)/shard_map/ppermute | solution.py:642
  14.1 1.0 copy-start.2
  15.0 0.9 copy-start.3
  16.0 0.9 copy-start.4
  16.9 0.9 copy-start.5
  17.8 0.8 copy-start.6
  18.5 0.8 copy-start.7
  19.3 0.8 copy-start.8
  47.5 13.4 %copy-start = (f32[16,32,512]{2,1,0:T(8,128)S(1)}, f32[16,32,512]{2,1,0:T(8,128)}, u32[]{:S(2)}) copy-start(f32[16,32,512]{2,1,0:T(8,128)} %param.10) | copy-start | bytes 3145732

commit v3 on v2

--- a/solution.py
+++ b/solution.py
@@ -95,25 +95,60 @@
     return keys, loads
 
 
+VMEM_BYTES = 67043328
+
+
+def device_of(index):
+    ny, nz = lax.axis_size("gy"), lax.axis_size("gz")
+    return {"gx": index // (ny * nz), "gy": (index // nz) % ny, "gz": index % nz}
+
+
 def surface_kernel(
-    begin_ref, low_ref, high_ref, positions_ref, normals_ref, tension_ref, weight_ref,
-    owner_ref, cell_ref, connect_ref, force_ref, packed_ref,
-    wide, jumps, turned, lists, counted, counted_scalar, sem,
+    positions_hbm, normals_hbm, tension_hbm, weight_hbm, owner_hbm, cell_hbm, connect_hbm,
+    force_ref, got_ref,
+    positions_ref, normals_ref, tension_ref, weight_ref, owner_ref, cell_ref, connect_ref,
+    low_ref, high_ref, packed_ref, wide, jumps, turned, lists, below_ref, counted, counted_scalar,
+    load_sems, sem, edge_send, edge_recv, all_send, all_recv,
 ):
     npoint = positions_ref.shape[1]
     nrow = npoint // LANES
     nowner = packed_ref.shape[0]
-    begin, total = begin_ref[0], begin_ref[1]
+    total = npoint * nowner
+    me = lax.axis_index(("gx", "gy", "gz"))
+    begin = me * npoint
+    sources = (positions_hbm, connect_hbm, weight_hbm, normals_hbm, tension_hbm, owner_hbm, cell_hbm)
+    targets = (positions_ref, connect_ref, weight_ref, normals_ref, tension_ref, owner_ref, cell_ref)
+    reads = [
+        pltpu.make_async_copy(source, target, load_sems.at[which])
+        for which, (source, target) in enumerate(zip(sources, targets))
+    ]
+    for read in reads:
+        read.start()
+
+    barrier = pltpu.get_barrier_semaphore()
+
+    def greet(offset, carry):
+        pl.semaphore_signal(
+            barrier, inc=1, device_id=device_of((me + offset) % nowner),
+            device_id_type=pl.DeviceIdType.MESH,
+        )
+        return carry
+
+    lax.fori_loop(1, nowner, greet, 0)
+    for read in reads:
+        read.wait()
+
     half = lax.broadcasted_iota(jnp.int32, (3, LANES), 1) < HALO
-    before = pltpu.roll(low_ref[...], HALO, 1)
-    for row in range(nrow + 1):
-        source = high_ref[...] if row == nrow else positions_ref[:, row * LANES : (row + 1) * LANES]
-        after = pltpu.roll(source, HALO, 1)
+    first_block = pltpu.roll(positions_ref[:, 0:LANES], HALO, 1)
+    before = first_block
+    for row in range(1, nrow):
+        after = pltpu.roll(positions_ref[:, row * LANES : (row + 1) * LANES], HALO, 1)
         wide[0:3, row * LANES : (row + 1) * LANES] = jnp.where(half, before, after)
         before = after
+    last_block = before
 
     def one_row(row, carry):
-        at = pl.multiple_of(row * LANES, LANES)
+        at = row * LANES if isinstance(row, int) else pl.multiple_of(row * LANES, LANES)
         here, there = pl.ds(at, LANES), pl.ds(at + LANES, LANES)
         blank = jnp.zeros((2, LANES), jnp.int32)
         index = jnp.concatenate([connect_ref[:, here], blank], axis=0)
@@ -134,7 +169,24 @@
         jumps[pl.ds(row, 1), :] = jump
         return carry
 
-    lax.fori_loop(0, nrow, one_row, 0, unroll=8)
+    lax.fori_loop(0, (nrow - 2) // 2, lambda i, c: one_row(2 * i + 2, one_row(2 * i + 1, c)), 0, unroll=4)
+
+    pl.semaphore_wait(barrier, nowner - 1)
+    edges = (
+        (positions_ref.at[:, pl.ds(npoint - LANES, LANES)], low_ref, 1),
+        (positions_ref.at[:, pl.ds(0, LANES)], high_ref, nowner - 1),
+    )
+    sends = []
+    for which, (source, target, offset) in enumerate(edges):
+        sends.append(
+            pltpu.make_async_remote_copy(
+                src_ref=source, dst_ref=target,
+                send_sem=edge_send.at[which], recv_sem=edge_recv.at[which],
+                device_id=device_of((me + offset) % nowner), device_id_type=pl.DeviceIdType.MESH,
+            )
+        )
+    for send in sends:
+        send.start()
 
     ranks = lax.broadcasted_iota(jnp.int32, (nowner, LANES), 0)
 
@@ -143,10 +195,18 @@
         return below + jnp.where(names < ranks, 1, 0)
 
     below = lax.fori_loop(0, nrow, count_row, jnp.zeros((nowner, LANES), jnp.int32), unroll=4)
-    starts = jnp.sum(below.astype(jnp.float32), axis=1, keepdims=True)
-    turned[...] = jnp.broadcast_to(starts, (nowner, LANES))
-    counted[...] = jnp.transpose(turned[...])[0:8, :].astype(jnp.int32)
+    for bit in range(7):
+        below = below + pltpu.roll(below, 1 << bit, 1)
+    below_ref[...] = below
+    counted[...] = jnp.transpose(below_ref[...])[0:8, :]
     fetch = pltpu.make_async_copy(counted, counted_scalar, sem)
+
+    for send in sends:
+        send.wait()
+    wide[0:3, 0:LANES] = jnp.where(half, pltpu.roll(low_ref[...], HALO, 1), first_block)
+    wide[0:3, npoint : npoint + LANES] = jnp.where(half, last_block, pltpu.roll(high_ref[...], HALO, 1))
+    one_row(0, 0)
+    one_row(nrow - 1, 0)
 
     keys, loads = [], []
     for tile in range(nrow // 8):
@@ -165,6 +225,7 @@
             if which == 0:
                 value = (value & ((1 << CELL_BITS) - 1)).astype(jnp.float32)
             turned[pl.ds(tile, 8, stride=8), :] = value
+        turned[64:128, :] = jnp.zeros((64, LANES), jnp.float32)
         flipped = jnp.transpose(turned[...])
         turned[...] = flipped
         even = turned[pl.ds(0, 64, stride=2), :]
@@ -192,11 +253,35 @@
 
     lax.fori_loop(0, nowner, one_owner, 0, unroll=8)
 
+    def send_one(offset, carry):
+        other = (me + offset) % nowner
+        pltpu.make_async_remote_copy(
+            src_ref=packed_ref.at[other], dst_ref=got_ref.at[me],
+            send_sem=all_send, recv_sem=all_recv,
+            device_id=device_of(other), device_id_type=pl.DeviceIdType.MESH,
+        ).start()
+        return carry
+
+    lax.fori_loop(1, nowner, send_one, 0)
+    keep = pltpu.make_async_copy(packed_ref.at[me], got_ref.at[me], sem)
+    keep.start()
+    everything = pltpu.make_async_remote_copy(
+        src_ref=packed_ref.at[pl.ds(0, nowner - 1)], dst_ref=got_ref.at[pl.ds(0, nowner - 1)],
+        send_sem=all_send, recv_sem=all_recv,
+        device_id=device_of((me + 1) % nowner), device_id_type=pl.DeviceIdType.MESH,
+    )
+    everything.wait_send()
+    everything.wait_recv()
+    keep.wait()
+
 
 def spread_kernel(
-    got_ref, rhs_ref, forcing_ref,
-    keys_scratch, loads_scratch, grid, turned, bounds, bounds_scalar, work, sem,
+    got_ref, rhs_hbm, force_in, forcing_ref, force_ref,
+    keys_scratch, loads_scratch, grid, turned, bounds, bounds_scalar, work, rhs_ref, sem, rhs_sem,
 ):
+    read = pltpu.make_async_copy(rhs_hbm, rhs_ref, rhs_sem)
+    read.start()
+    force_ref[...] = force_in[...]
     nsender = got_ref.shape[0] // 4
     ngroup = nsender // 32
     places = [("l", 1 << bit) for bit in range(7)] + [("v", 1), ("v", 2), ("v", 4)]
@@ -288,6 +373,7 @@
 
     lax.fori_loop(0, (filled + BATCH - 1) // BATCH, one_batch, 0)
 
+    read.wait()
     shape = forcing_ref.shape
     for plane in range(shape[0]):
         for part in range(shape[2] // LANES):
@@ -299,8 +385,10 @@
 BATCH = 8
 
 
-def surface_and_pack(begin, low, high, positions, normals, tension, edge_weight, owners, cells, connectivity, nowner):
+def surface_and_send(positions, normals, tension, edge_weight, owners, cells, connectivity):
+    nowner = lax.axis_size(("gx", "gy", "gz"))
     vmem = pl.BlockSpec(memory_space=pltpu.VMEM)
+    arrays = (positions, normals, tension, edge_weight, owners, cells, connectivity)
     return pl.pallas_call(
         surface_kernel,
         name="surface",
@@ -308,29 +396,44 @@
             jax.ShapeDtypeStruct(positions.shape, jnp.float32),
             jax.ShapeDtypeStruct((nowner, 4, LANES), jnp.float32),
         ),
-        in_specs=[pl.BlockSpec(memory_space=pltpu.SMEM)] + [vmem] * 9,
-        out_specs=(vmem, vmem),
-        scratch_shapes=[
+        in_specs=[pl.BlockSpec(memory_space=pltpu.HBM)] * len(arrays),
+        out_specs=(vmem, pl.BlockSpec(memory_space=pltpu.HBM)),
+        scratch_shapes=[pltpu.VMEM(array.shape, array.dtype) for array in arrays]
+        + [
+            pltpu.VMEM((3, LANES), jnp.float32),
+            pltpu.VMEM((3, LANES), jnp.float32),
+            pltpu.VMEM((nowner, 4, LANES), jnp.float32),
             pltpu.VMEM((8, positions.shape[1] + LANES), jnp.float32),
             pltpu.VMEM((positions.shape[1] // LANES, LANES), jnp.float32),
             pltpu.VMEM((128, LANES), jnp.float32),
             pltpu.VMEM((144, LANES), jnp.float32),
+            pltpu.VMEM((nowner, LANES), jnp.int32),
             pltpu.VMEM((8, LANES), jnp.int32),
             pltpu.SMEM((8, LANES), jnp.int32),
+            pltpu.SemaphoreType.DMA((7,)),
+            pltpu.SemaphoreType.DMA,
+            pltpu.SemaphoreType.DMA((2,)),
+            pltpu.SemaphoreType.DMA((2,)),
+            pltpu.SemaphoreType.DMA,
             pltpu.SemaphoreType.DMA,
         ],
-        compiler_params=pltpu.CompilerParams(vmem_limit_bytes=32 * 1024 * 1024),
-    )(begin, low, high, positions, normals, tension, edge_weight, owners, cells, connectivity)
-
-
-def spread_cells(got, pressure_rhs):
+        compiler_params=pltpu.CompilerParams(
+            vmem_limit_bytes=VMEM_BYTES, collective_id=1, has_side_effects=True
+        ),
+    )(*arrays)
+
+
+def spread_cells(got, pressure_rhs, force):
     vmem = pl.BlockSpec(memory_space=pltpu.VMEM)
     return pl.pallas_call(
         spread_kernel,
         name="spread",
-        out_shape=jax.ShapeDtypeStruct(pressure_rhs.shape, jnp.float32),
-        in_specs=[vmem, vmem],
-        out_specs=vmem,
+        out_shape=(
+            jax.ShapeDtypeStruct(pressure_rhs.shape, jnp.float32),
+            jax.ShapeDtypeStruct(force.shape, jnp.float32),
+        ),
+        in_specs=[vmem, pl.BlockSpec(memory_space=pltpu.HBM), vmem],
+        out_specs=(vmem, vmem),
         scratch_shapes=[
             pltpu.VMEM((2, 128, LANES), jnp.int32),
             pltpu.VMEM((2, 128, LANES), jnp.float32),
@@ -339,10 +442,12 @@
             pltpu.VMEM((8, LANES), jnp.int32),
             pltpu.SMEM((8, LANES), jnp.int32),
             pltpu.SMEM((512,), jnp.int32),
+            pltpu.VMEM(pressure_rhs.shape, jnp.float32),
+            pltpu.SemaphoreType.DMA,
             pltpu.SemaphoreType.DMA,
         ],
-        compiler_params=pltpu.CompilerParams(vmem_limit_bytes=32 * 1024 * 1024),
-    )(got, pressure_rhs)
+        compiler_params=pltpu.CompilerParams(vmem_limit_bytes=VMEM_BYTES),
+    )(got, pressure_rhs, force)
 
 
 AXES = ("gx", "gy", "gz")
@@ -368,10 +473,16 @@
 
 
 def cycle_kernel(
-    plane_rows, forcing_ref, shift_ref, pressure_ref,
+    plane_rows, forcing_hbm, shift_hbm, pressure_ref, forcing_ref, shift_ref,
     wide_a, wide_b, coarse_a, coarse_b, inverse, update, coarse_rhs, coarse_inverse, coarse_update,
-    rows_out, rows_in, columns_out, columns_in, send_sems, recv_sems,
+    rows_out, rows_in, columns_out, columns_in, send_sems, recv_sems, load_sems,
 ):
+    reads = [
+        pltpu.make_async_copy(source, target, load_sems.at[which])
+        for which, (source, target) in enumerate(((forcing_hbm, forcing_ref), (shift_hbm, shift_ref)))
+    ]
+    for read in reads:
+        read.start()
     width = forcing_ref.shape[1]
     nplane = forcing_ref.shape[0] // plane_rows
     ncoarse = nplane // 2
@@ -402,7 +513,8 @@
                     barrier, inc=1, device_id={axis: there}, device_id_type=pl.DeviceIdType.MESH
                 )
 
-    pl.semaphore_wait(barrier, neighbours)
+    for read in reads:
+        read.wait()
 
     lane = lax.broadcasted_iota(jnp.int32, (8, LANES), 1)
 
@@ -513,6 +625,7 @@
 
     edges = each_plane(nplane, first_step)
     slot = 0
+    pl.semaphore_wait(barrier, neighbours)
     exchange_faces(wide[slot], nplane, slot, *edges)
     for sweep_index in range(SMOOTH - 1):
         keep, gain = gains[sweep_index]
@@ -598,9 +711,11 @@
         functools.partial(cycle_kernel, rows),
         name="multigrid",
         out_shape=jax.ShapeDtypeStruct(flat, f32),
-        in_specs=[vmem, vmem],
+        in_specs=[pl.BlockSpec(memory_space=pltpu.HBM)] * 2,
         out_specs=vmem,
         scratch_shapes=[
+            pltpu.VMEM(flat, f32),
+            pltpu.VMEM(flat, f32),
             pltpu.VMEM((flat[0] + 2 * rows, width), f32),
             pltpu.VMEM((flat[0] + 2 * rows, width), f32),
             pltpu.VMEM((half[0] + 2 * rows, width), f32),
@@ -616,9 +731,10 @@
             pltpu.VMEM((2, 2, 8, LANES), f32),
             pltpu.SemaphoreType.DMA((2, 6)),
             pltpu.SemaphoreType.DMA((2, 6)),
+            pltpu.SemaphoreType.DMA((2,)),
         ],
         compiler_params=pltpu.CompilerParams(
-            vmem_limit_bytes=48 * 1024 * 1024, collective_id=0, has_side_effects=True
+            vmem_limit_bytes=VMEM_BYTES, collective_id=0, has_side_effects=True
         ),
     )(forcing.reshape(flat), shift_diag.reshape(flat)).reshape(forcing.shape)
 
@@ -634,28 +750,18 @@
     cell_map,
     connectivity,
 ):
-    every = ("gx", "gy", "gz")
-    npoint = positions.shape[1]
-    ndevice = lax.axis_size(every)
-    begin = lax.axis_index(every) * npoint
-    up = [(i, (i + 1) % ndevice) for i in range(ndevice)]
-    low = lax.ppermute(positions[:, npoint - LANES :], every, up)
-    high = lax.ppermute(positions[:, :LANES], every, [(b, a) for a, b in up])
-    surface_force, packed = surface_and_pack(
-        jnp.stack([begin, npoint * ndevice]).astype(jnp.int32),
-        low,
-        high,
+    ndevice = lax.axis_size(("gx", "gy", "gz"))
+    nrow = positions.shape[1] // LANES
+    force, got = surface_and_send(
         positions,
         normals,
-        tension.reshape(npoint // LANES, LANES),
+        tension.reshape(nrow, LANES),
         edge_weight,
-        owner_map.reshape(npoint // LANES, LANES),
-        cell_map.reshape(npoint // LANES, LANES),
+        owner_map.reshape(nrow, LANES),
+        cell_map.reshape(nrow, LANES),
         connectivity,
-        ndevice,
     )
-    got = lax.all_to_all(packed, every, split_axis=0, concat_axis=0, tiled=True)
-    forcing = spread_cells(got.reshape(4 * ndevice, LANES), pressure_rhs)
+    forcing, surface_force = spread_cells(got.reshape(4 * ndevice, LANES), pressure_rhs, force)
     pressure = multigrid(forcing, shift_diag)
     return (pressure, surface_force)
 

time: 115 us -> 102 us (0.89)
  Pallas kernels: 73.4 us -> 98.8 us
  blocking collectives: 19.6 us -> 0 us
  starting transfers between devices: 6.31 us -> 0 us
  waiting for transfers between devices: 6.25 us -> 0 us
  local copies, waits for them, and re-layouts: 7.75 us -> 2.29 us
    pallas_call x2, Pallas kernels: 21.3 us -> 44.2 us  [the longest x1 28.8 us: surface_and_send(): pl.pallas_call(surface_kernel, name='surface', out_shape=(jax.ShapeDtypeS...]
    all_to_all x1 -> x0, blocking collectives: 19.6 us -> none  [body(): got = lax.all_to_all(packed, every, split_axis=0, concat_axis=0, tiled=True)]
    ppermute x2 -> x0, starting transfers between devices: 6.31 us -> none  [the longest x1 6.31 us: body(): high = lax.ppermute(positions[:, :LANES], every, [(b, a) for a, b in up])]
    ppermute x2 -> x0, waiting for transfers between devices: 6.25 us -> none  [the longest x1 5.59 us: body(): low = lax.ppermute(positions[:, npoint - LANES:], every, up)]
    unnamed x19 -> x1, local copies, waits for them, and re-layouts: 6.96 us -> 2.29 us
    pallas_call x1, Pallas kernels: 52.2 us -> 54.6 us  [multigrid(): pl.pallas_call(functools.partial(cycle_kernel, rows), name='multigrid', o...]
  transfers between devices with their start and end apart: 2 -> 0, of which waited for: 2 -> 0; matrix products, arithmetic and copies ran while one was open for 0% -> 0% of each run, Pallas kernels for 0% -> 0%
where the time goes in v3:
time: 102 us
  Pallas kernels  98.8 us (97%)
  local copies, waits for them, and re-layouts  2.29 us (2%)
    pallas_call x1, Pallas kernels, multigrid(): pl.pallas_call(functools.partial(cycle_kernel, rows), name='multigrid', o...  54.6 us
    pallas_call x1, Pallas kernels, surface_and_send(): pl.pallas_call(surface_kernel, name='surface', out_shape=(jax.ShapeDtypeS...  28.8 us
    pallas_call x1, Pallas kernels, spread_cells(): pl.pallas_call(spread_kernel, name='spread', out_shape=(jax.ShapeDtypeStr...  15.4 us
    unnamed x1, local copies, waits for them, and re-layouts  2.29 us

profile of v3, /device:TPU:1, one launch (start us, length us, event | category | flops | bytes accessed | tf_op | source)
XLA Modules:
  0.0 101.8 jit_solution(10207972098571304389)
XLA Ops:
  0.6 28.8 %surface.1 = (f32[3,8192]{1,0:T(4,128)}, f32[128,4,128]{2,1,0:T(4,128)}) custom-call(f32[3,8192]{1,0:T(4,128)} %positions_hbm.1, f32[3,8192]{1,0:T(4,128)} %normals_hbm.1, f32[64,128]{1,0:T(8,128)} %bitcast.11, f32[6,8192]{1,0:T(8,128)} %weight_hbm.1, s32[64,128]{1,0:T(8,128)} %bitcast.12, s32[64,128]{1,0:T(8,128)} %bitcast.13, s32[6,8192]{1,0:T(8,128)} %connect_hbm.1), custom_call_target="tpu_custom_call" | custom-call | tf_op jit(solution)/shard_map/surface/pallas_call | solution.py:392
  29.4 15.4 %spread.1 = (f32[16,32,512]{2,1,0:T(8,128)}, f32[3,8192]{1,0:T(4,128)}) custom-call(f32[512,128]{1,0:T(8,128)} %bitcast.10, f32[16,32,512]{2,1,0:T(8,128)} %rhs_hbm.1, f32[3,8192]{1,0:T(4,128)} %get-tuple-element.7.force_in), custom_call_target="tpu_custom_call" | custom-call | tf_op jit(solution)/shard_map/spread/pallas_call | solution.py:428
  44.9 54.6 %multigrid.1 = f32[512,512]{1,0:T(8,128)} custom-call(f32[512,512]{1,0:T(8,128)} %bitcast.9, f32[512,512]{1,0:T(8,128)} %bitcast.8), custom_call_target="tpu_custom_call" | custom-call | tf_op jit(solution)/shard_map/multigrid/pallas_call | solution.py:710
  99.5 2.3 %copy.12 = f32[16,32,512]{2,1,0:T(8,128)} copy(f32[16,32,512]{2,1,0:T(8,128)} %bitcast.7) | data formatting | bytes 2097152

commit v4 on v3

--- a/solution.py
+++ b/solution.py
@@ -87,12 +87,12 @@
     return new_keys, new_loads
 
 
-def merge_levels(keys, loads, places, first, last):
+def merge_levels(groups, places, first, last):
     for level in range(first, last + 1):
-        keys, loads = exchange(keys, loads, places, range(level + 1), level)
+        groups = [exchange(*group, places, range(level + 1), level) for group in groups]
         for bit in reversed(range(level)):
-            keys, loads = exchange(keys, loads, places, (bit,), bit)
-    return keys, loads
+            groups = [exchange(*group, places, (bit,), bit) for group in groups]
+    return groups
 
 
 VMEM_BYTES = 67043328
@@ -201,6 +201,25 @@
     counted[...] = jnp.transpose(below_ref[...])[0:8, :]
     fetch = pltpu.make_async_copy(counted, counted_scalar, sem)
 
+    keys, loads = [], []
+    for tile in range(nrow // 8):
+        rows = slice(8 * tile, 8 * tile + 8)
+        cell = cell_ref[rows, :]
+        cell = ((cell & 384) << 9) | ((cell >> 9) << 7) | (cell & 127)
+        key = ((owner_ref[rows, :] << CELL_BITS) | cell) << 1
+        load = jumps[rows, :]
+        if tile in (0, nrow // 8 - 1):
+            line = lax.broadcasted_iota(jnp.int32, (8, LANES), 0)
+            lane = lax.broadcasted_iota(jnp.int32, (8, LANES), 1)
+            late = line == (7 if tile else 0)
+            key = key | jnp.where(late, 1, 0)
+            load = jnp.where(late, (lane + (LANES if tile else 0)).astype(jnp.float32), load)
+        keys.append(key)
+        loads.append(load)
+    fetch.start()
+    places = [("v", 1), ("v", 2), ("v", 4), ("s", 1), ("s", 2), ("s", 4)]
+    places += [("l", 1 << bit) for bit in range(7)]
+    ((keys, loads),) = merge_levels([(keys, loads)], places, 0, 12)
     for send in sends:
         send.wait()
     wide[0:3, 0:LANES] = jnp.where(half, pltpu.roll(low_ref[...], HALO, 1), first_block)
@@ -208,17 +227,15 @@
     one_row(0, 0)
     one_row(nrow - 1, 0)
 
-    keys, loads = [], []
+    first_jumps = jnp.broadcast_to(jumps[0:1, :], (8, LANES))
+    last_jumps = jnp.broadcast_to(jumps[nrow - 1 : nrow, :], (8, LANES))
     for tile in range(nrow // 8):
-        rows = slice(8 * tile, 8 * tile + 8)
-        cell = cell_ref[rows, :]
-        cell = ((cell & 384) << 9) | ((cell >> 9) << 7) | (cell & 127)
-        keys.append((owner_ref[rows, :] << CELL_BITS) | cell)
-        loads.append(jumps[rows, :])
-    fetch.start()
-    places = [("v", 1), ("v", 2), ("v", 4), ("s", 1), ("s", 2), ("s", 4)]
-    places += [("l", 1 << bit) for bit in range(7)]
-    keys, loads = merge_levels(keys, loads, places, 0, 12)
+        late = (keys[tile] & 1) == 1
+        which = jnp.where(late, loads[tile], 0.0).astype(jnp.int32)
+        lane = which & (LANES - 1)
+        value = jnp.where(which >= LANES, pick(last_jumps, lane, 1), pick(first_jumps, lane, 1))
+        loads[tile] = jnp.where(late, value, loads[tile])
+        keys[tile] = keys[tile] >> 1
     for which, arrays in ((0, keys), (1, loads)):
         for tile in range(8):
             value = arrays[tile]
@@ -276,11 +293,9 @@
 
 
 def spread_kernel(
-    got_ref, rhs_hbm, force_in, forcing_ref, force_ref,
-    keys_scratch, loads_scratch, grid, turned, bounds, bounds_scalar, work, rhs_ref, sem, rhs_sem,
+    got_ref, force_in, grid, force_ref,
+    keys_scratch, loads_scratch, turned, bounds, bounds_scalar, work, sem,
 ):
-    read = pltpu.make_async_copy(rhs_hbm, rhs_ref, rhs_sem)
-    read.start()
     force_ref[...] = force_in[...]
     nsender = got_ref.shape[0] // 4
     ngroup = nsender // 32
@@ -293,14 +308,16 @@
 
     lax.fori_loop(0, grid.shape[0] // 64, zero, 0)
 
-    def one_group(group):
+    def read_group(group):
         keys, loads = [], []
         for quarter in range(4):
             for side in range(2):
                 first = (group * 32 + quarter * 8) * 4 + 2 * side
                 keys.append(got_ref[pl.ds(first, 8, stride=4), :])
                 loads.append(got_ref[pl.ds(first + 1, 8, stride=4), :])
-        keys, loads = merge_levels(keys, loads, places, 8, 12)
+        return keys, loads
+
+    def store_group(group, keys, loads):
         for quarter in range(4):
             rows = pl.ds(group * 32 + quarter, 8, stride=4)
             last = jnp.full((8, 1), -1, jnp.int32)
@@ -321,8 +338,11 @@
             pair = jnp.where(last < 0, 0, base) * 32 + repeats
             turned[rows, :] = jnp.broadcast_to(pair.astype(jnp.float32), (8, LANES))
 
-    for group in range(ngroup):
-        one_group(group)
+    for first in range(0, ngroup, TOGETHER):
+        chosen = range(first, first + TOGETHER)
+        merged = merge_levels([read_group(group) for group in chosen], places, 8, 12)
+        for group, (keys, loads) in zip(chosen, merged):
+            store_group(group, keys, loads)
     bounds[...] = jnp.transpose(turned[...])[0:8, :].astype(jnp.int32)
     fetch = pltpu.make_async_copy(bounds, bounds_scalar, sem)
     fetch.start()
@@ -373,16 +393,9 @@
 
     lax.fori_loop(0, (filled + BATCH - 1) // BATCH, one_batch, 0)
 
-    read.wait()
-    shape = forcing_ref.shape
-    for plane in range(shape[0]):
-        for part in range(shape[2] // LANES):
-            columns = slice(part * LANES, (part + 1) * LANES)
-            first = (part * shape[0] + plane) * shape[1]
-            forcing_ref[plane, :, columns] = rhs_ref[plane, :, columns] + grid[first : first + shape[1], :]
-
-
-BATCH = 8
+
+BATCH = 16
+TOGETHER = 4
 
 
 def surface_and_send(positions, normals, tension, edge_weight, owners, cells, connectivity):
@@ -423,31 +436,29 @@
     )(*arrays)
 
 
-def spread_cells(got, pressure_rhs, force):
+def spread_cells(got, force, ncell):
     vmem = pl.BlockSpec(memory_space=pltpu.VMEM)
     return pl.pallas_call(
         spread_kernel,
         name="spread",
         out_shape=(
-            jax.ShapeDtypeStruct(pressure_rhs.shape, jnp.float32),
+            jax.ShapeDtypeStruct((ncell // LANES + 128, LANES), jnp.float32),
             jax.ShapeDtypeStruct(force.shape, jnp.float32),
         ),
-        in_specs=[vmem, pl.BlockSpec(memory_space=pltpu.HBM), vmem],
+        in_specs=[vmem, vmem],
         out_specs=(vmem, vmem),
         scratch_shapes=[
             pltpu.VMEM((2, 128, LANES), jnp.int32),
             pltpu.VMEM((2, 128, LANES), jnp.float32),
-            pltpu.VMEM((2048 + 128, LANES), jnp.float32),
             pltpu.VMEM((128, LANES), jnp.float32),
             pltpu.VMEM((8, LANES), jnp.int32),
             pltpu.SMEM((8, LANES), jnp.int32),
             pltpu.SMEM((512,), jnp.int32),
-            pltpu.VMEM(pressure_rhs.shape, jnp.float32),
-            pltpu.SemaphoreType.DMA,
             pltpu.SemaphoreType.DMA,
         ],
-        compiler_params=pltpu.CompilerParams(vmem_limit_bytes=VMEM_BYTES),
-    )(got, pressure_rhs, force)
+        cost_estimate=pl.CostEstimate(flops=10**10, bytes_accessed=10**7, transcendentals=0),
+        compiler_params=pltpu.CompilerParams(vmem_limit_bytes=32 * 1024 * 1024),
+    )(got, force)
 
 
 AXES = ("gx", "gy", "gz")
@@ -473,16 +484,10 @@
 
 
 def cycle_kernel(
-    plane_rows, forcing_hbm, shift_hbm, pressure_ref, forcing_ref, shift_ref,
+    plane_rows, added_ref, rhs_ref, shift_ref, pressure_ref, forcing_ref,
     wide_a, wide_b, coarse_a, coarse_b, inverse, update, coarse_rhs, coarse_inverse, coarse_update,
-    rows_out, rows_in, columns_out, columns_in, send_sems, recv_sems, load_sems,
+    rows_out, rows_in, columns_out, columns_in, send_sems, recv_sems,
 ):
-    reads = [
-        pltpu.make_async_copy(source, target, load_sems.at[which])
-        for which, (source, target) in enumerate(((forcing_hbm, forcing_ref), (shift_hbm, shift_ref)))
-    ]
-    for read in reads:
-        read.start()
     width = forcing_ref.shape[1]
     nplane = forcing_ref.shape[0] // plane_rows
     ncoarse = nplane // 2
@@ -513,8 +518,6 @@
                     barrier, inc=1, device_id={axis: there}, device_id_type=pl.DeviceIdType.MESH
                 )
 
-    for read in reads:
-        read.wait()
 
     lane = lax.broadcasted_iota(jnp.int32, (8, LANES), 1)
 
@@ -587,7 +590,7 @@
     nothing = jnp.zeros((8, LANES), jnp.float32)
 
     def each_plane(count, step):
-        return lax.fori_loop(0, count, step, (nothing, nothing))
+        return lax.fori_loop(0, count, step, (nothing, nothing), unroll=8)
 
     def sweep(source, target, slot, count, reach, rhs, scale, change, keep, gain, out=None):
         def step(plane, carry):
@@ -618,7 +621,10 @@
         here = rows_of(plane)
         scale = 1.0 / (6.0 + shift_ref[here, :])
         inverse[here, :] = scale
-        answer = scale * forcing_ref[here, :] * (1.0 / centre)
+        added = [added_ref[rows_of(part * nplane + plane), :] for part in range(width // LANES)]
+        forcing = rhs_ref[here, :] + jnp.concatenate(added, axis=1)
+        forcing_ref[here, :] = forcing
+        answer = scale * forcing * (1.0 / centre)
         update[here, :] = answer
         wide_a[rows_of(plane + 1), :] = answer
         return columns_of(answer, plane, 0, *carry)
@@ -701,8 +707,8 @@
         slot = 1 - slot
 
 
-def multigrid(forcing, shift_diag):
-    planes, rows, width = forcing.shape
+def multigrid(added, pressure_rhs, shift_diag):
+    planes, rows, width = shift_diag.shape
     vmem = pl.BlockSpec(memory_space=pltpu.VMEM)
     flat = (planes * rows, width)
     half = (planes // 2 * rows, width)
@@ -711,10 +717,9 @@
         functools.partial(cycle_kernel, rows),
         name="multigrid",
         out_shape=jax.ShapeDtypeStruct(flat, f32),
-        in_specs=[pl.BlockSpec(memory_space=pltpu.HBM)] * 2,
+        in_specs=[vmem] * 3,
         out_specs=vmem,
         scratch_shapes=[
-            pltpu.VMEM(flat, f32),
             pltpu.VMEM(flat, f32),
             pltpu.VMEM((flat[0] + 2 * rows, width), f32),
             pltpu.VMEM((flat[0] + 2 * rows, width), f32),
@@ -731,12 +736,11 @@
             pltpu.VMEM((2, 2, 8, LANES), f32),
             pltpu.SemaphoreType.DMA((2, 6)),
             pltpu.SemaphoreType.DMA((2, 6)),
-            pltpu.SemaphoreType.DMA((2,)),
         ],
         compiler_params=pltpu.CompilerParams(
-            vmem_limit_bytes=VMEM_BYTES, collective_id=0, has_side_effects=True
+            vmem_limit_bytes=40 * 1024 * 1024, collective_id=0, has_side_effects=True
         ),
-    )(forcing.reshape(flat), shift_diag.reshape(flat)).reshape(forcing.shape)
+    )(added, pressure_rhs.reshape(flat), shift_diag.reshape(flat)).reshape(shift_diag.shape)
 
 
 def body(
@@ -761,8 +765,8 @@
         cell_map.reshape(nrow, LANES),
         connectivity,
     )
-    forcing, surface_force = spread_cells(got.reshape(4 * ndevice, LANES), pressure_rhs, force)
-    pressure = multigrid(forcing, shift_diag)
+    added, surface_force = spread_cells(got.reshape(4 * ndevice, LANES), force, pressure_rhs.size)
+    pressure = multigrid(added, pressure_rhs, shift_diag)
     return (pressure, surface_force)
 
 

time: 102 us -> 85.9 us (0.84)
  Pallas kernels: 98.8 us -> 82.5 us
    pallas_call x1, Pallas kernels: 54.6 us -> 41.9 us  [multigrid(): pl.pallas_call(functools.partial(cycle_kernel, rows), name='multigrid', o...]
    pallas_call x1, Pallas kernels: 28.8 us -> 26.7 us  [surface_and_send(): pl.pallas_call(surface_kernel, name='surface', out_shape=(jax.ShapeDtypeS...]
    pallas_call x1, Pallas kernels: 15.4 us -> 13.8 us  [spread_cells(): pl.pallas_call(spread_kernel, name='spread', out_shape=(jax.ShapeDtypeStr...]
    unnamed x1 -> x9, local copies, waits for them, and re-layouts: 2.29 us -> 2.83 us
where the time goes in v4:
time: 85.9 us; the launch traced here: 86 us
  Pallas kernels  82.5 us (96%)
  local copies, waits for them, and re-layouts  2.83 us (3%)
    pallas_call x1, Pallas kernels, multigrid(): pl.pallas_call(functools.partial(cycle_kernel, rows), name='multigrid', o...  41.9 us
    pallas_call x1, Pallas kernels, surface_and_send(): pl.pallas_call(surface_kernel, name='surface', out_shape=(jax.ShapeDtypeS...  26.7 us
    pallas_call x1, Pallas kernels, spread_cells(): pl.pallas_call(spread_kernel, name='spread', out_shape=(jax.ShapeDtypeStr...  13.8 us
    unnamed x9, local copies, waits for them, and re-layouts  2.83 us

profile of v4, /device:TPU:1, one launch (start us, length us, event | category | flops | bytes accessed | tf_op | source)
XLA Modules:
  0.0 86.0 jit_solution(12278946808313490831)
XLA Ops:
  0.6 26.7 %surface.1 = (f32[3,8192]{1,0:T(4,128)}, f32[128,4,128]{2,1,0:T(4,128)}) custom-call(f32[3,8192]{1,0:T(4,128)} %positions_hbm.1, f32[3,8192]{1,0:T(4,128)} %normals_hbm.1, f32[64,128]{1,0:T(8,128)} %bitcast.11, f32[6,8192]{1,0:T(8,128)} %weight_hbm.1, s32[64,128]{1,0:T(8,128)} %bitcast.12, s32[64,128]{1,0:T(8,128)} %bitcast.13, s32[6,8192]{1,0:T(8,128)} %connect_hbm.1), custom_call_target="tpu_custom_call" | custom-call | tf_op jit(solution)/shard_map/surface/pallas_call | solution.py:405
  27.4 0.0 copy-start.2
  27.4 0.9 %copy-done.2 = f32[128,4,128]{2,1,0:T(4,128)S(1)} copy-done((f32[128,4,128]{2,1,0:T(4,128)S(1)}, f32[128,4,128]{2,1,0:T(4,128)}, u32[]{:S(2)}) %copy-start.2) | copy-done | bytes 262168
  28.3 0.0 copy-start.3
  28.3 0.9 %copy-done.3 = f32[3,8192]{1,0:T(4,128)S(1)} copy-done((f32[3,8192]{1,0:T(4,128)S(1)}, f32[3,8192]{1,0:T(4,128)}, u32[]{:S(2)}) %copy-start.3) | copy-done | bytes 98328
  29.2 0.0 copy-start
  29.2 0.0 copy-start.1
  29.2 13.8 %spread.1 = (f32[2176,128]{1,0:T(8,128)S(1)}, f32[3,8192]{1,0:T(4,128)}) custom-call(f32[512,128]{1,0:T(8,128)S(1)} %bitcast.10, f32[3,8192]{1,0:T(4,128)S(1)} %copy-done.3), custom_call_target="tpu_custom_call" | custom-call | flops 10000000000 | bytes 10000000 | tf_op jit(solution)/shard_map/spread/pallas_call | solution.py:441
  43.0 0.0 copy-done
  43.0 0.0 copy-done.1
  43.1 41.9 %multigrid.1 = f32[512,512]{1,0:T(8,128)S(1)} custom-call(f32[2176,128]{1,0:T(8,128)S(1)} %get-tuple-element.8.added_ref, f32[512,512]{1,0:T(8,128)S(1)} %bitcast.8, f32[512,512]{1,0:T(8,128)S(1)} %bitcast.9), custom_call_target="tpu_custom_call" | custom-call | tf_op jit(solution)/shard_map/multigrid/pallas_call | solution.py:716
  85.0 1.0 %copy.12 = f32[16,32,512]{2,1,0:T(8,128)} copy(f32[16,32,512]{2,1,0:T(8,128)S(1)} %bitcast.7) | data formatting | bytes 2097152
Async XLA Ops:
  27.4 1.0 %copy-start.2 = (f32[128,4,128]{2,1,0:T(4,128)S(1)}, f32[128,4,128]{2,1,0:T(4,128)}, u32[]{:S(2)}) copy-start(f32[128,4,128]{2,1,0:T(4,128)} %get-tuple-element.6) | copy-start | bytes 786436
  28.3 0.9 %copy-start.3 = (f32[3,8192]{1,0:T(4,128)S(1)}, f32[3,8192]{1,0:T(4,128)}, u32[]{:S(2)}) copy-start(f32[3,8192]{1,0:T(4,128)} %get-tuple-element.7.force_in) | copy-start | bytes 294916
  29.2 13.8 %copy-start = (f32[16,32,512]{2,1,0:T(8,128)S(1)}, f32[16,32,512]{2,1,0:T(8,128)}, u32[]{:S(2)}) copy-start(f32[16,32,512]{2,1,0:T(8,128)} %param.9) | copy-start | bytes 3145732
  29.2 13.8 %copy-start.1 = (f32[16,32,512]{2,1,0:T(8,128)S(1)}, f32[16,32,512]{2,1,0:T(8,128)}, u32[]{:S(2)}) copy-start(f32[16,32,512]{2,1,0:T(8,128)} %param.10) | copy-start | bytes 3145732

commit v5 on v4

--- a/solution.py
+++ b/solution.py
@@ -521,17 +521,20 @@
 
     lane = lax.broadcasted_iota(jnp.int32, (8, LANES), 1)
 
+    def pack_columns(head, tail, plane, low, high):
+        for tile in range(tiles):
+            rows = slice(8 * tile, 8 * tile + 8)
+            mine = lane == plane * tiles + tile
+            first = pick(head[rows, :], jnp.zeros((8, LANES), jnp.int32), 1)
+            last = pick(tail[rows, :], jnp.full((8, LANES), LANES - 1, jnp.int32), 1)
+            low = jnp.where(mine, first, low)
+            high = jnp.where(mine, last, high)
+        return low, high
+
     def columns_of(field, plane, slot, low, high):
         rows_out[slot, 0, pl.ds(plane, 1), :] = field[0:1, :]
         rows_out[slot, 1, pl.ds(plane, 1), :] = field[plane_rows - 1 : plane_rows, :]
-        for tile in range(tiles):
-            rows = slice(8 * tile, 8 * tile + 8)
-            mine = lane == plane * tiles + tile
-            first = pick(field[rows, 0:LANES], jnp.zeros((8, LANES), jnp.int32), 1)
-            last = pick(field[rows, width - LANES : width], jnp.full((8, LANES), LANES - 1, jnp.int32), 1)
-            low = jnp.where(mine, first, low)
-            high = jnp.where(mine, last, high)
-        return low, high
+        return pack_columns(field[:, 0:LANES], field[:, width - LANES : width], plane, low, high)
 
     def exchange_faces(field, count, slot, low, high):
         columns_out[slot, 0] = low
@@ -552,63 +555,113 @@
         copies = halo_copies(sides, slot, send_sems, recv_sems)
         for copy, sends, receives in copies:
             pl.when(sends)(copy.start)
-        for copy, sends, receives in copies:
-            pl.when(sends)(copy.wait_send)
-            pl.when(receives)(copy.wait_recv)
+
+        def finish():
+            for copy, sends, receives in copies:
+                pl.when(sends)(copy.wait_send)
+                pl.when(receives)(copy.wait_recv)
+
+        return finish
 
     row_index = lax.broadcasted_iota(jnp.int32, (plane_rows, width), 0)
     lane_index = lax.broadcasted_iota(jnp.int32, (plane_rows, LANES), 1)
 
-    def beside(field, plane, slot, reach):
-        first = pl.multiple_of((plane + 1) * plane_rows, plane_rows)
-        centre_plane = field[pl.ds(first, plane_rows), :]
-        total = field[pl.ds(first - plane_rows, plane_rows), :] + field[pl.ds(first + plane_rows, plane_rows), :]
-        above = rows_in[slot, 0, pl.ds(plane, 1), :]
-        below = rows_in[slot, 1, pl.ds(plane, 1), :]
-        total = total + jnp.where(row_index < reach, above, pltpu.roll(centre_plane, reach, 0))
+    def beside(field, plane, count, reach):
+        first = (plane + 1) * plane_rows
+        if not isinstance(plane, int):
+            first = pl.multiple_of(first, plane_rows)
+        middle = field[pl.ds(first, plane_rows), :]
+        total = jnp.where(row_index < reach, 0.0, pltpu.roll(middle, reach, 0))
         total = total + jnp.where(
-            row_index >= plane_rows - reach, below, pltpu.roll(centre_plane, plane_rows - reach, 0)
+            row_index >= plane_rows - reach, 0.0, pltpu.roll(middle, plane_rows - reach, 0)
         )
-        spread_low, spread_high = [], []
-        for tile in range(tiles):
-            where = jnp.full((8, LANES), plane * tiles + tile, jnp.int32)
-            spread_low.append(pick(columns_in[slot, 0], where, 1))
-            spread_high.append(pick(columns_in[slot, 1], where, 1))
-        left = pltpu.roll(centre_plane, reach, 1)
-        right = pltpu.roll(centre_plane, width - reach, 1)
-        left_edge = jnp.where(lane_index < reach, jnp.concatenate(spread_low, axis=0), left[:, :LANES])
-        right_edge = jnp.where(
-            lane_index >= LANES - reach, jnp.concatenate(spread_high, axis=0), right[:, width - LANES :]
-        )
+        if not isinstance(plane, int) or plane > 0:
+            total = total + field[pl.ds(first - plane_rows, plane_rows), :]
+        if not isinstance(plane, int) or plane < count - 1:
+            total = total + field[pl.ds(first + plane_rows, plane_rows), :]
+        left = pltpu.roll(middle, reach, 1)
+        right = pltpu.roll(middle, width - reach, 1)
+        left_edge = jnp.where(lane_index < reach, 0.0, left[:, :LANES])
+        right_edge = jnp.where(lane_index >= LANES - reach, 0.0, right[:, width - LANES :])
         total = total + jnp.concatenate([left_edge, left[:, LANES:]], axis=1)
         total = total + jnp.concatenate([right[:, : width - LANES], right_edge], axis=1)
-        return centre_plane, total
+        return middle, total
+
+    def correct(source, target, padding, slot, count, reach, scale, gain, change, packed):
+        def apply(first, number, columns, value):
+            here, there = pl.ds(first, number), pl.ds(first + padding, number)
+            moved = value if scale is None else (gain * scale[here, columns]) * value
+            if change is not None:
+                change[here, columns] = change[here, columns] + moved
+            answer = target[there, columns] + moved
+            target[there, columns] = answer
+            return answer
+
+        entire, head, tail = slice(0, width), slice(0, LANES), slice(width - LANES, width)
+        apply(0, plane_rows, entire, source[0:plane_rows, :])
+        apply(
+            (count - 1) * plane_rows, plane_rows, entire,
+            source[(count + 1) * plane_rows : (count + 2) * plane_rows, :],
+        )
+
+        def step(plane, carry):
+            base = pl.multiple_of(plane * plane_rows, plane_rows)
+            for row in range(reach):
+                apply(base + row, 1, entire, rows_in[slot, 0, pl.ds(plane, 1), :])
+                apply(base + plane_rows - 1 - row, 1, entire, rows_in[slot, 1, pl.ds(plane, 1), :])
+            low, high = [], []
+            for tile in range(tiles):
+                where = jnp.full((8, LANES), plane * tiles + tile, jnp.int32)
+                low.append(pick(columns_in[slot, 0], where, 1))
+                high.append(pick(columns_in[slot, 1], where, 1))
+            low = jnp.where(lane_index < reach, jnp.concatenate(low, axis=0), 0.0)
+            high = jnp.where(lane_index >= LANES - reach, jnp.concatenate(high, axis=0), 0.0)
+            first = apply(base, plane_rows, head, low)
+            last = apply(base, plane_rows, tail, high)
+            if not packed:
+                return carry
+            for side, row in ((0, 0), (1, plane_rows - 1)):
+                rows_out[1 - slot, side, pl.ds(plane, 1), :] = target[pl.ds(base + padding + row, 1), :]
+            return pack_columns(first, last, plane, *carry)
+
+        return lax.fori_loop(0, count, step, (nothing, nothing), unroll=8)
+
+    nothing = jnp.zeros((8, LANES), jnp.float32)
 
     def rows_of(plane):
+        if isinstance(plane, int):
+            return pl.ds(plane * plane_rows, plane_rows)
         return pl.ds(pl.multiple_of(plane * plane_rows, plane_rows), plane_rows)
-
-    nothing = jnp.zeros((8, LANES), jnp.float32)
 
     def each_plane(count, step):
         return lax.fori_loop(0, count, step, (nothing, nothing), unroll=8)
 
-    def sweep(source, target, slot, count, reach, rhs, scale, change, keep, gain, out=None):
+    def inner_planes(count, step):
+        step(0, 0)
+        lax.fori_loop(1, count - 1, step, 0, unroll=(count - 2) // 2)
+        step(count - 1, 0)
+
+    def sweep(source, target, slot, edges, count, reach, rhs, scale, change, keep, gain, out=None):
+        finish = exchange_faces(source, count, slot, *edges)
+
         def step(plane, carry):
             here = rows_of(plane)
-            field, total = beside(source, plane, slot, reach)
-            remain = scale[here, :] * (rhs[here, :] + total) - field
-            moved = gain * remain
+            field, total = beside(source, plane, count, reach)
+            moved = gain * (scale[here, :] * (rhs[here, :] + total) - field)
             if keep:
                 moved = moved + keep * change[here, :]
-            answer = field + moved
             if out is not None:
-                out[here, :] = answer
-                return carry
-            change[here, :] = moved
-            target[rows_of(plane + 1), :] = answer
-            return columns_of(answer, plane, 1 - slot, *carry)
-
-        return each_plane(count, step)
+                out[here, :] = field + moved
+            else:
+                change[here, :] = moved
+                target[rows_of(plane + 1), :] = field + moved
+            return carry
+
+        inner_planes(count, step)
+        finish()
+        if out is not None:
+            return correct(source, out, 0, slot, count, reach, scale, gain, None, False)
+        return correct(source, target, plane_rows, slot, count, reach, scale, gain, change, True)
 
     ratio = centre / spread
     gains, factor = [], 1.0 / ratio
@@ -632,15 +685,13 @@
     edges = each_plane(nplane, first_step)
     slot = 0
     pl.semaphore_wait(barrier, neighbours)
-    exchange_faces(wide[slot], nplane, slot, *edges)
     for sweep_index in range(SMOOTH - 1):
         keep, gain = gains[sweep_index]
         edges = sweep(
-            wide[slot], wide[1 - slot], slot, nplane, 1, forcing_ref, inverse, update, keep, gain
+            wide[slot], wide[1 - slot], slot, edges, nplane, 1, forcing_ref, inverse, update, keep, gain
         )
         slot = 1 - slot
-        exchange_faces(wide[slot], nplane, slot, *edges)
-    smooth = wide[slot]
+    smooth, remains_ref = wide[slot], wide[1 - slot]
 
     lane_pair = lax.broadcasted_iota(jnp.int32, (8, LANES), 1) ^ 1
     line_pair = lax.broadcasted_iota(jnp.int32, (8, LANES), 0) ^ 1
@@ -656,19 +707,22 @@
             lines.append(jnp.concatenate(parts, axis=1))
         return jnp.concatenate(lines, axis=0)
 
-    smooth_slot = slot
+    finish = exchange_faces(smooth, nplane, slot, *edges)
+
+    def leave(plane, carry):
+        here = rows_of(plane)
+        field, total = beside(smooth, plane, nplane, 1)
+        remains_ref[rows_of(plane + 1), :] = forcing_ref[here, :] - ((6.0 + shift_ref[here, :]) * field - total)
+        return carry
+
+    inner_planes(nplane, leave)
+    finish()
+    correct(smooth, remains_ref, plane_rows, slot, nplane, 1, None, 1.0, None, False)
     slot = 1 - slot
 
     def restrict(plane, carry):
-        remains, shifts = None, None
-        for half in range(2):
-            fine = 2 * plane + half
-            here = rows_of(fine)
-            field, total = beside(smooth, fine, smooth_slot, 1)
-            shift = shift_ref[here, :]
-            remain = forcing_ref[here, :] - ((6.0 + shift) * field - total)
-            remains = remain if remains is None else remains + remain
-            shifts = shift if shifts is None else shifts + shift
+        remains = remains_ref[rows_of(2 * plane + 1), :] + remains_ref[rows_of(2 * plane + 2), :]
+        shifts = shift_ref[rows_of(2 * plane), :] + shift_ref[rows_of(2 * plane + 1), :]
         rhs = 0.5 * pair_sum(remains)
         scale = 1.0 / (6.0 + 0.5 * pair_sum(shifts))
         answer = scale * rhs * (1.0 / centre)
@@ -681,10 +735,9 @@
 
     edges = each_plane(ncoarse, restrict)
     for sweep_index in range(COARSE_SMOOTH - 1):
-        exchange_faces(coarse[slot], ncoarse, slot, *edges)
         keep, gain = gains[sweep_index]
         edges = sweep(
-            coarse[slot], coarse[1 - slot], slot, ncoarse, 2,
+            coarse[slot], coarse[1 - slot], slot, edges, ncoarse, 2,
             coarse_rhs, coarse_inverse, coarse_update, keep, gain,
         )
         slot = 1 - slot
@@ -698,10 +751,9 @@
 
     edges = each_plane(nplane, begin_again)
     for sweep_index in range(SMOOTH):
-        exchange_faces(wide[slot], nplane, slot, *edges)
         keep, gain = gains[sweep_index - 1] if sweep_index else (0.0, 1.0 / centre)
         edges = sweep(
-            wide[slot], wide[1 - slot], slot, nplane, 1, forcing_ref, inverse, update, keep, gain,
+            wide[slot], wide[1 - slot], slot, edges, nplane, 1, forcing_ref, inverse, update, keep, gain,
             pressure_ref if sweep_index == SMOOTH - 1 else None,
         )
         slot = 1 - slot

time: 85.9 us -> 77.6 us (0.903)
  Pallas kernels: 82.5 us -> 73.6 us
    pallas_call x1, Pallas kernels: 41.9 us -> 35.4 us  [multigrid(): pl.pallas_call(functools.partial(cycle_kernel, rows), name='multigrid', o...]
    pallas_call x1, Pallas kernels: 13.8 us -> 11.5 us  [spread_cells(): pl.pallas_call(spread_kernel, name='spread', out_shape=(jax.ShapeDtypeStr...]
where the time goes in v5:
time: 77.6 us; the launch traced here: 77.1 us
  Pallas kernels  73.6 us (95%)
  local copies, waits for them, and re-layouts  2.83 us (4%)
    pallas_call x1, Pallas kernels, multigrid(): pl.pallas_call(functools.partial(cycle_kernel, rows), name='multigrid', o...  35.4 us
    pallas_call x1, Pallas kernels, surface_and_send(): pl.pallas_call(surface_kernel, name='surface', out_shape=(jax.ShapeDtypeS...  26.7 us
    pallas_call x1, Pallas kernels, spread_cells(): pl.pallas_call(spread_kernel, name='spread', out_shape=(jax.ShapeDtypeStr...  11.5 us
    unnamed x9, local copies, waits for them, and re-layouts  2.83 us

profile of v5, /device:TPU:1, one launch (start us, length us, event | category | flops | bytes accessed | tf_op | source)
XLA Modules:
  0.0 77.1 jit_solution(17184724800735000722)
XLA Ops:
  0.6 26.7 %surface.1 = (f32[3,8192]{1,0:T(4,128)}, f32[128,4,128]{2,1,0:T(4,128)}) custom-call(f32[3,8192]{1,0:T(4,128)} %positions_hbm.1, f32[3,8192]{1,0:T(4,128)} %normals_hbm.1, f32[64,128]{1,0:T(8,128)} %bitcast.11, f32[6,8192]{1,0:T(8,128)} %weight_hbm.1, s32[64,128]{1,0:T(8,128)} %bitcast.12, s32[64,128]{1,0:T(8,128)} %bitcast.13, s32[6,8192]{1,0:T(8,128)} %connect_hbm.1), custom_call_target="tpu_custom_call" | custom-call | tf_op jit(solution)/shard_map/surface/pallas_call | solution.py:405
  27.4 0.0 copy-start.2
  27.4 0.9 %copy-done.2 = f32[128,4,128]{2,1,0:T(4,128)S(1)} copy-done((f32[128,4,128]{2,1,0:T(4,128)S(1)}, f32[128,4,128]{2,1,0:T(4,128)}, u32[]{:S(2)}) %copy-start.2) | copy-done | bytes 262168
  28.3 0.0 copy-start.3
  28.3 0.9 %copy-done.3 = f32[3,8192]{1,0:T(4,128)S(1)} copy-done((f32[3,8192]{1,0:T(4,128)S(1)}, f32[3,8192]{1,0:T(4,128)}, u32[]{:S(2)}) %copy-start.3) | copy-done | bytes 98328
  29.2 0.0 copy-start
  29.2 0.0 copy-start.1
  29.2 11.5 %spread.1 = (f32[2176,128]{1,0:T(8,128)S(1)}, f32[3,8192]{1,0:T(4,128)}) custom-call(f32[512,128]{1,0:T(8,128)S(1)} %bitcast.10, f32[3,8192]{1,0:T(4,128)S(1)} %copy-done.3), custom_call_target="tpu_custom_call" | custom-call | flops 10000000000 | bytes 10000000 | tf_op jit(solution)/shard_map/spread/pallas_call | solution.py:441
  40.7 0.0 copy-done
  40.7 0.0 copy-done.1
  40.7 35.4 %multigrid.1 = f32[512,512]{1,0:T(8,128)S(1)} custom-call(f32[2176,128]{1,0:T(8,128)S(1)} %get-tuple-element.8.added_ref, f32[512,512]{1,0:T(8,128)S(1)} %bitcast.8, f32[512,512]{1,0:T(8,128)S(1)} %bitcast.9), custom_call_target="tpu_custom_call" | custom-call | tf_op jit(solution)/shard_map/multigrid/pallas_call | solution.py:768
  76.1 1.0 %copy.12 = f32[16,32,512]{2,1,0:T(8,128)} copy(f32[16,32,512]{2,1,0:T(8,128)S(1)} %bitcast.7) | data formatting | bytes 2097152
Async XLA Ops:
  27.4 1.0 %copy-start.2 = (f32[128,4,128]{2,1,0:T(4,128)S(1)}, f32[128,4,128]{2,1,0:T(4,128)}, u32[]{:S(2)}) copy-start(f32[128,4,128]{2,1,0:T(4,128)} %get-tuple-element.6) | copy-start | bytes 786436
  28.3 0.9 %copy-start.3 = (f32[3,8192]{1,0:T(4,128)S(1)}, f32[3,8192]{1,0:T(4,128)}, u32[]{:S(2)}) copy-start(f32[3,8192]{1,0:T(4,128)} %get-tuple-element.7.force_in) | copy-start | bytes 294916
  29.2 11.5 %copy-start = (f32[16,32,512]{2,1,0:T(8,128)S(1)}, f32[16,32,512]{2,1,0:T(8,128)}, u32[]{:S(2)}) copy-start(f32[16,32,512]{2,1,0:T(8,128)} %param.9) | copy-start | bytes 3145732
  29.2 11.5 %copy-start.1 = (f32[16,32,512]{2,1,0:T(8,128)S(1)}, f32[16,32,512]{2,1,0:T(8,128)}, u32[]{:S(2)}) copy-start(f32[16,32,512]{2,1,0:T(8,128)} %param.10) | copy-start | bytes 3145732

commit v6 on v5

--- a/solution.py
+++ b/solution.py
@@ -105,10 +105,10 @@
 
 def surface_kernel(
     positions_hbm, normals_hbm, tension_hbm, weight_hbm, owner_hbm, cell_hbm, connect_hbm,
-    force_ref, got_ref,
+    got_ref,
     positions_ref, normals_ref, tension_ref, weight_ref, owner_ref, cell_ref, connect_ref,
-    low_ref, high_ref, packed_ref, wide, jumps, turned, lists, below_ref, counted, counted_scalar,
-    load_sems, sem, edge_send, edge_recv, all_send, all_recv,
+    low_ref, high_ref, packed_ref, force_ref, wide, jumps, turned, lists, below_ref, counted, counted_scalar,
+    load_sems, sem, keep_sem, edge_send, edge_recv, all_send, all_recv,
 ):
     npoint = positions_ref.shape[1]
     nrow = npoint // LANES
@@ -164,7 +164,7 @@
             taken = jnp.where(second, pick(upper, index, 1), pick(lower, index, 1))
             pulled = weight * (taken - positions_ref[axis : axis + 1, here])
             force = strength * jnp.sum(pulled, axis=0, keepdims=True)
-            force_ref[axis : axis + 1, here] = force
+            force_ref[row, axis : axis + 1, :] = force
             jump = jump + force * normals_ref[axis : axis + 1, here]
         jumps[pl.ds(row, 1), :] = jump
         return carry
@@ -226,6 +226,7 @@
     wide[0:3, npoint : npoint + LANES] = jnp.where(half, last_block, pltpu.roll(high_ref[...], HALO, 1))
     one_row(0, 0)
     one_row(nrow - 1, 0)
+    hand_on = pltpu.make_async_copy(force_ref, got_ref.at[pl.ds(nowner, nrow)], keep_sem)
 
     first_jumps = jnp.broadcast_to(jumps[0:1, :], (8, LANES))
     last_jumps = jnp.broadcast_to(jumps[nrow - 1 : nrow, :], (8, LANES))
@@ -268,20 +269,34 @@
         packed_ref[owner] = block[0:4, :]
         return carry
 
-    lax.fori_loop(0, nowner, one_owner, 0, unroll=8)
-
-    def send_one(offset, carry):
-        other = (me + offset) % nowner
+    def send_to(other):
         pltpu.make_async_remote_copy(
             src_ref=packed_ref.at[other], dst_ref=got_ref.at[me],
             send_sem=all_send, recv_sem=all_recv,
             device_id=device_of(other), device_id_type=pl.DeviceIdType.MESH,
         ).start()
+
+    def pack_some(step, carry):
+        for piece in range(8):
+            one_owner((me + 8 * step + piece) % nowner, 0)
         return carry
 
-    lax.fori_loop(1, nowner, send_one, 0)
+    def pack_and_send(step, carry):
+        pack_some(step, carry)
+        for piece in range(8):
+            send_to((me + 8 * (step - 1) + piece) % nowner)
+        return carry
+
+    pack_some(0, 0)
+    pack_some(1, 0)
+    for piece in range(1, 8):
+        send_to((me + piece) % nowner)
+    lax.fori_loop(2, nowner // 8, pack_and_send, 0)
+    for piece in range(8):
+        send_to((me + nowner - 8 + piece) % nowner)
     keep = pltpu.make_async_copy(packed_ref.at[me], got_ref.at[me], sem)
     keep.start()
+    hand_on.start()
     everything = pltpu.make_async_remote_copy(
         src_ref=packed_ref.at[pl.ds(0, nowner - 1)], dst_ref=got_ref.at[pl.ds(0, nowner - 1)],
         send_sem=all_send, recv_sem=all_recv,
@@ -290,14 +305,18 @@
     everything.wait_send()
     everything.wait_recv()
     keep.wait()
+    hand_on.wait()
 
 
 def spread_kernel(
-    got_ref, force_in, grid, force_ref,
+    got_ref, grid, force_ref,
     keys_scratch, loads_scratch, turned, bounds, bounds_scalar, work, sem,
 ):
-    force_ref[...] = force_in[...]
-    nsender = got_ref.shape[0] // 4
+    nrow = force_ref.shape[1] // LANES
+    nsender = got_ref.shape[0] // 4 - nrow
+    for row in range(nrow):
+        first = 4 * (nsender + row)
+        force_ref[:, row * LANES : (row + 1) * LANES] = got_ref[first : first + 3, :]
     ngroup = nsender // 32
     places = [("l", 1 << bit) for bit in range(7)] + [("v", 1), ("v", 2), ("v", 4)]
     places += [("s", 1), ("s", 2), ("s", 4)]
@@ -400,22 +419,19 @@
 
 def surface_and_send(positions, normals, tension, edge_weight, owners, cells, connectivity):
     nowner = lax.axis_size(("gx", "gy", "gz"))
-    vmem = pl.BlockSpec(memory_space=pltpu.VMEM)
     arrays = (positions, normals, tension, edge_weight, owners, cells, connectivity)
     return pl.pallas_call(
         surface_kernel,
         name="surface",
-        out_shape=(
-            jax.ShapeDtypeStruct(positions.shape, jnp.float32),
-            jax.ShapeDtypeStruct((nowner, 4, LANES), jnp.float32),
-        ),
+        out_shape=jax.ShapeDtypeStruct((nowner + tension.shape[0], 4, LANES), jnp.float32),
         in_specs=[pl.BlockSpec(memory_space=pltpu.HBM)] * len(arrays),
-        out_specs=(vmem, pl.BlockSpec(memory_space=pltpu.HBM)),
+        out_specs=pl.BlockSpec(memory_space=pltpu.HBM),
         scratch_shapes=[pltpu.VMEM(array.shape, array.dtype) for array in arrays]
         + [
             pltpu.VMEM((3, LANES), jnp.float32),
             pltpu.VMEM((3, LANES), jnp.float32),
             pltpu.VMEM((nowner, 4, LANES), jnp.float32),
+            pltpu.VMEM((tension.shape[0], 4, LANES), jnp.float32),
             pltpu.VMEM((8, positions.shape[1] + LANES), jnp.float32),
             pltpu.VMEM((positions.shape[1] // LANES, LANES), jnp.float32),
             pltpu.VMEM((128, LANES), jnp.float32),
@@ -424,6 +440,7 @@
             pltpu.VMEM((8, LANES), jnp.int32),
             pltpu.SMEM((8, LANES), jnp.int32),
             pltpu.SemaphoreType.DMA((7,)),
+            pltpu.SemaphoreType.DMA,
             pltpu.SemaphoreType.DMA,
             pltpu.SemaphoreType.DMA((2,)),
             pltpu.SemaphoreType.DMA((2,)),
@@ -436,16 +453,16 @@
     )(*arrays)
 
 
-def spread_cells(got, force, ncell):
+def spread_cells(got, npoint, ncell):
     vmem = pl.BlockSpec(memory_space=pltpu.VMEM)
     return pl.pallas_call(
         spread_kernel,
         name="spread",
         out_shape=(
             jax.ShapeDtypeStruct((ncell // LANES + 128, LANES), jnp.float32),
-            jax.ShapeDtypeStruct(force.shape, jnp.float32),
+            jax.ShapeDtypeStruct((3, npoint), jnp.float32),
         ),
-        in_specs=[vmem, vmem],
+        in_specs=[vmem],
         out_specs=(vmem, vmem),
         scratch_shapes=[
             pltpu.VMEM((2, 128, LANES), jnp.int32),
@@ -458,7 +475,7 @@
         ],
         cost_estimate=pl.CostEstimate(flops=10**10, bytes_accessed=10**7, transcendentals=0),
         compiler_params=pltpu.CompilerParams(vmem_limit_bytes=32 * 1024 * 1024),
-    )(got, force)
+    )(got)
 
 
 AXES = ("gx", "gy", "gz")
@@ -806,9 +823,8 @@
     cell_map,
     connectivity,
 ):
-    ndevice = lax.axis_size(("gx", "gy", "gz"))
     nrow = positions.shape[1] // LANES
-    force, got = surface_and_send(
+    got = surface_and_send(
         positions,
         normals,
         tension.reshape(nrow, LANES),
@@ -817,7 +833,7 @@
         cell_map.reshape(nrow, LANES),
         connectivity,
     )
-    added, surface_force = spread_cells(got.reshape(4 * ndevice, LANES), force, pressure_rhs.size)
+    added, surface_force = spread_cells(got.reshape(-1, LANES), positions.shape[1], pressure_rhs.size)
     pressure = multigrid(added, pressure_rhs, shift_diag)
     return (pressure, surface_force)
 

time: 77.6 us -> 74.1 us (0.955); the launches traced: 77.1 us -> 74.7 us
  Pallas kernels: 73.6 us -> 72 us
  local copies, waits for them, and re-layouts: 2.83 us -> 1.97 us
    pallas_call x1, Pallas kernels: 26.7 us -> 24.7 us  [surface_and_send(): pl.pallas_call(surface_kernel, name='surface', out_shape=jax.ShapeDtypeSt...]
    pallas_call x1, Pallas kernels: 11.5 us -> 12.6 us  [spread_cells(): pl.pallas_call(spread_kernel, name='spread', out_shape=(jax.ShapeDtypeStr...]
    unnamed x9 -> x7, local copies, waits for them, and re-layouts: 2.83 us -> 1.97 us
where the time goes in v6:
time: 74.1 us; the launch traced here: 74.7 us
  Pallas kernels  72 us (97%)
  local copies, waits for them, and re-layouts  1.97 us (3%)
    pallas_call x1, Pallas kernels, multigrid(): pl.pallas_call(functools.partial(cycle_kernel, rows), name='multigrid', o...  34.7 us
    pallas_call x1, Pallas kernels, surface_and_send(): pl.pallas_call(surface_kernel, name='surface', out_shape=jax.ShapeDtypeSt...  24.7 us
    pallas_call x1, Pallas kernels, spread_cells(): pl.pallas_call(spread_kernel, name='spread', out_shape=(jax.ShapeDtypeStr...  12.6 us
    unnamed x7, local copies, waits for them, and re-layouts  1.97 us

profile of v6, /device:TPU:1, one launch (start us, length us, event | category | flops | bytes accessed | tf_op | source)
XLA Modules:
  0.0 74.7 jit_solution(8993396902437539320)
XLA Ops:
  0.6 24.7 %surface.1 = f32[192,4,128]{2,1,0:T(4,128)} custom-call(f32[3,8192]{1,0:T(4,128)} %positions_hbm.1, f32[3,8192]{1,0:T(4,128)} %normals_hbm.1, f32[64,128]{1,0:T(8,128)} %bitcast.11, f32[6,8192]{1,0:T(8,128)} %weight_hbm.1, s32[64,128]{1,0:T(8,128)} %bitcast.12, s32[64,128]{1,0:T(8,128)} %bitcast.13, s32[6,8192]{1,0:T(8,128)} %connect_hbm.1), custom_call_target="tpu_custom_call" | custom-call | tf_op jit(solution)/shard_map/surface/pallas_call | solution.py:423
  25.4 0.0 copy-start.2
  25.4 1.0 %copy-done.2 = f32[192,4,128]{2,1,0:T(4,128)S(1)} copy-done((f32[192,4,128]{2,1,0:T(4,128)S(1)}, f32[192,4,128]{2,1,0:T(4,128)}, u32[]{:S(2)}) %copy-start.2) | copy-done | bytes 393240
  26.4 0.0 copy-start
  26.4 0.0 copy-start.1
  26.4 12.6 %spread.1 = (f32[2176,128]{1,0:T(8,128)S(1)}, f32[3,8192]{1,0:T(4,128)}) custom-call(f32[768,128]{1,0:T(8,128)S(1)} %bitcast.10), custom_call_target="tpu_custom_call" | custom-call | flops 10000000000 | bytes 10000000 | tf_op jit(solution)/shard_map/spread/pallas_call | solution.py:458
  39.0 0.0 copy-done
  39.0 0.0 copy-done.1
  39.0 34.7 %multigrid.1 = f32[512,512]{1,0:T(8,128)S(1)} custom-call(f32[2176,128]{1,0:T(8,128)S(1)} %get-tuple-element.4.added_ref, f32[512,512]{1,0:T(8,128)S(1)} %bitcast.8, f32[512,512]{1,0:T(8,128)S(1)} %bitcast.9), custom_call_target="tpu_custom_call" | custom-call | tf_op jit(solution)/shard_map/multigrid/pallas_call | solution.py:785
  73.7 1.0 %copy.12 = f32[16,32,512]{2,1,0:T(8,128)} copy(f32[16,32,512]{2,1,0:T(8,128)S(1)} %bitcast.7) | data formatting | bytes 2097152
Async XLA Ops:
  25.4 1.0 %copy-start.2 = (f32[192,4,128]{2,1,0:T(4,128)S(1)}, f32[192,4,128]{2,1,0:T(4,128)}, u32[]{:S(2)}) copy-start(f32[192,4,128]{2,1,0:T(4,128)} %surface.1) | copy-start | bytes 1179652
  26.4 12.6 %copy-start = (f32[16,32,512]{2,1,0:T(8,128)S(1)}, f32[16,32,512]{2,1,0:T(8,128)}, u32[]{:S(2)}) copy-start(f32[16,32,512]{2,1,0:T(8,128)} %param.9) | copy-start | bytes 3145732
  26.4 12.6 %copy-start.1 = (f32[16,32,512]{2,1,0:T(8,128)S(1)}, f32[16,32,512]{2,1,0:T(8,128)}, u32[]{:S(2)}) copy-start(f32[16,32,512]{2,1,0:T(8,128)} %param.10) | copy-start | bytes 3145732

commit v7 on v6

--- a/solution.py
+++ b/solution.py
@@ -553,9 +553,7 @@
         rows_out[slot, 1, pl.ds(plane, 1), :] = field[plane_rows - 1 : plane_rows, :]
         return pack_columns(field[:, 0:LANES], field[:, width - LANES : width], plane, low, high)
 
-    def exchange_faces(field, count, slot, low, high):
-        columns_out[slot, 0] = low
-        columns_out[slot, 1] = high
+    def face_copies(field, count, slot):
         here = pl.ds(0, count)
 
         def planes(first):
@@ -569,9 +567,17 @@
             ("gz", -1, columns_out.at[slot, 0], columns_in.at[slot, 1]),
             ("gz", 1, columns_out.at[slot, 1], columns_in.at[slot, 0]),
         )
-        copies = halo_copies(sides, slot, send_sems, recv_sems)
+        return halo_copies(sides, slot, send_sems, recv_sems)
+
+    def start_all(copies):
         for copy, sends, receives in copies:
             pl.when(sends)(copy.start)
+
+    def exchange_faces(field, count, slot, started, low, high):
+        columns_out[slot, 0] = low
+        columns_out[slot, 1] = high
+        copies = face_copies(field, count, slot)
+        start_all(copies[2:] if started else copies)
 
         def finish():
             for copy, sends, receives in copies:
@@ -622,7 +628,9 @@
         )
 
         def step(plane, carry):
-            base = pl.multiple_of(plane * plane_rows, plane_rows)
+            base = plane * plane_rows
+            if not isinstance(plane, int):
+                base = pl.multiple_of(base, plane_rows)
             for row in range(reach):
                 apply(base + row, 1, entire, rows_in[slot, 0, pl.ds(plane, 1), :])
                 apply(base + plane_rows - 1 - row, 1, entire, rows_in[slot, 1, pl.ds(plane, 1), :])
@@ -641,7 +649,12 @@
                 rows_out[1 - slot, side, pl.ds(plane, 1), :] = target[pl.ds(base + padding + row, 1), :]
             return pack_columns(first, last, plane, *carry)
 
-        return lax.fori_loop(0, count, step, (nothing, nothing), unroll=8)
+        edges = (nothing, nothing)
+        for plane in (0, count - 1, 1, 2):
+            edges = step(plane, edges)
+        if packed:
+            start_all(face_copies(target, count, 1 - slot)[:2])
+        return lax.fori_loop(3, count - 1, step, edges, unroll=min(6, count - 4))
 
     nothing = jnp.zeros((8, LANES), jnp.float32)
 
@@ -655,11 +668,11 @@
 
     def inner_planes(count, step):
         step(0, 0)
-        lax.fori_loop(1, count - 1, step, 0, unroll=(count - 2) // 2)
+        lax.fori_loop(1, count - 1, step, 0, unroll=2)
         step(count - 1, 0)
 
-    def sweep(source, target, slot, edges, count, reach, rhs, scale, change, keep, gain, out=None):
-        finish = exchange_faces(source, count, slot, *edges)
+    def sweep(source, target, slot, edges, count, reach, rhs, scale, change, keep, gain, started, onward, out=None):
+        finish = exchange_faces(source, count, slot, started, *edges)
 
         def step(plane, carry):
             here = rows_of(plane)
@@ -678,7 +691,7 @@
         finish()
         if out is not None:
             return correct(source, out, 0, slot, count, reach, scale, gain, None, False)
-        return correct(source, target, plane_rows, slot, count, reach, scale, gain, change, True)
+        return correct(source, target, plane_rows, slot, count, reach, scale, gain, change, onward)
 
     ratio = centre / spread
     gains, factor = [], 1.0 / ratio
@@ -705,7 +718,8 @@
     for sweep_index in range(SMOOTH - 1):
         keep, gain = gains[sweep_index]
         edges = sweep(
-            wide[slot], wide[1 - slot], slot, edges, nplane, 1, forcing_ref, inverse, update, keep, gain
+            wide[slot], wide[1 - slot], slot, edges, nplane, 1, forcing_ref, inverse, update, keep, gain,
+            sweep_index > 0, True,
         )
         slot = 1 - slot
     smooth, remains_ref = wide[slot], wide[1 - slot]
@@ -724,7 +738,7 @@
             lines.append(jnp.concatenate(parts, axis=1))
         return jnp.concatenate(lines, axis=0)
 
-    finish = exchange_faces(smooth, nplane, slot, *edges)
+    finish = exchange_faces(smooth, nplane, slot, True, *edges)
 
     def leave(plane, carry):
         here = rows_of(plane)
@@ -756,6 +770,7 @@
         edges = sweep(
             coarse[slot], coarse[1 - slot], slot, edges, ncoarse, 2,
             coarse_rhs, coarse_inverse, coarse_update, keep, gain,
+            sweep_index > 0, sweep_index < COARSE_SMOOTH - 2,
         )
         slot = 1 - slot
     fix = coarse[slot]
@@ -771,7 +786,7 @@
         keep, gain = gains[sweep_index - 1] if sweep_index else (0.0, 1.0 / centre)
         edges = sweep(
             wide[slot], wide[1 - slot], slot, edges, nplane, 1, forcing_ref, inverse, update, keep, gain,
-            pressure_ref if sweep_index == SMOOTH - 1 else None,
+            sweep_index > 0, True, pressure_ref if sweep_index == SMOOTH - 1 else None,
         )
         slot = 1 - slot
 

time: 74.1 us -> 73.2 us (0.988)
  Pallas kernels: 72 us -> 70.5 us
    pallas_call x1, Pallas kernels: 34.7 us -> 33.7 us  [multigrid(): pl.pallas_call(functools.partial(cycle_kernel, rows), name='multigrid', o...]
where the time goes in v7:
time: 73.2 us
  Pallas kernels  70.5 us (96%)
  local copies, waits for them, and re-layouts  1.97 us (3%)
    pallas_call x1, Pallas kernels, multigrid(): pl.pallas_call(functools.partial(cycle_kernel, rows), name='multigrid', o...  33.7 us
    pallas_call x1, Pallas kernels, surface_and_send(): pl.pallas_call(surface_kernel, name='surface', out_shape=jax.ShapeDtypeSt...  24.7 us
    pallas_call x1, Pallas kernels, spread_cells(): pl.pallas_call(spread_kernel, name='spread', out_shape=(jax.ShapeDtypeStr...  12.1 us
    unnamed x7, local copies, waits for them, and re-layouts  1.97 us

profile of v7, /device:TPU:1, one launch (start us, length us, event | category | flops | bytes accessed | tf_op | source)
XLA Modules:
  0.0 73.2 jit_solution(7365581153382007860)
XLA Ops:
  0.6 24.7 %surface.1 = f32[192,4,128]{2,1,0:T(4,128)} custom-call(f32[3,8192]{1,0:T(4,128)} %positions_hbm.1, f32[3,8192]{1,0:T(4,128)} %normals_hbm.1, f32[64,128]{1,0:T(8,128)} %bitcast.11, f32[6,8192]{1,0:T(8,128)} %weight_hbm.1, s32[64,128]{1,0:T(8,128)} %bitcast.12, s32[64,128]{1,0:T(8,128)} %bitcast.13, s32[6,8192]{1,0:T(8,128)} %connect_hbm.1), custom_call_target="tpu_custom_call" | custom-call | tf_op jit(solution)/shard_map/surface/pallas_call | solution.py:423
  25.4 0.0 copy-start.2
  25.4 1.0 %copy-done.2 = f32[192,4,128]{2,1,0:T(4,128)S(1)} copy-done((f32[192,4,128]{2,1,0:T(4,128)S(1)}, f32[192,4,128]{2,1,0:T(4,128)}, u32[]{:S(2)}) %copy-start.2) | copy-done | bytes 393240
  26.4 0.0 copy-start
  26.4 0.0 copy-start.1
  26.4 12.1 %spread.1 = (f32[2176,128]{1,0:T(8,128)S(1)}, f32[3,8192]{1,0:T(4,128)}) custom-call(f32[768,128]{1,0:T(8,128)S(1)} %bitcast.10), custom_call_target="tpu_custom_call" | custom-call | flops 10000000000 | bytes 10000000 | tf_op jit(solution)/shard_map/spread/pallas_call | solution.py:458
  38.5 0.0 copy-done
  38.5 0.0 copy-done.1
  38.5 33.7 %multigrid.1 = f32[512,512]{1,0:T(8,128)S(1)} custom-call(f32[2176,128]{1,0:T(8,128)S(1)} %get-tuple-element.4.added_ref, f32[512,512]{1,0:T(8,128)S(1)} %bitcast.8, f32[512,512]{1,0:T(8,128)S(1)} %bitcast.9), custom_call_target="tpu_custom_call" | custom-call | tf_op jit(solution)/shard_map/multigrid/pallas_call | solution.py:800
  72.2 1.0 %copy.12 = f32[16,32,512]{2,1,0:T(8,128)} copy(f32[16,32,512]{2,1,0:T(8,128)S(1)} %bitcast.7) | data formatting | bytes 2097152
Async XLA Ops:
  25.4 1.0 %copy-start.2 = (f32[192,4,128]{2,1,0:T(4,128)S(1)}, f32[192,4,128]{2,1,0:T(4,128)}, u32[]{:S(2)}) copy-start(f32[192,4,128]{2,1,0:T(4,128)} %surface.1) | copy-start | bytes 1179652
  26.4 12.1 %copy-start = (f32[16,32,512]{2,1,0:T(8,128)S(1)}, f32[16,32,512]{2,1,0:T(8,128)}, u32[]{:S(2)}) copy-start(f32[16,32,512]{2,1,0:T(8,128)} %param.9) | copy-start | bytes 3145732
  26.4 12.1 %copy-start.1 = (f32[16,32,512]{2,1,0:T(8,128)S(1)}, f32[16,32,512]{2,1,0:T(8,128)}, u32[]{:S(2)}) copy-start(f32[16,32,512]{2,1,0:T(8,128)} %param.10) | copy-start | bytes 3145732
